TPU v7x, 32 devices: a whole 2x2x4 slice. The times are simulated.
32 devices in a mesh: grp: 2 (over y), row: 4 (over x, core), sub: 4 (over z).
Axes of the slice: x: 2, y: 2, z: 4, core: 2. Of those that a mesh axis runs over, the one named last changes fastest.
Arguments:
- residual_in: float32 [4, 2048, 2048], P('grp', ('row', 'sub')), parts along dimension 0, may hold values from -100 to 100
- direction: float32 [4, 2048, 2048], P('grp', ('row', 'sub')), parts along dimension 0, may hold values from -100 to 100
- spectrum: float32 [8192, 4096], P('grp', ('row', 'sub')), parts along dimension 0, may hold values from 0.0999 to 10.001, as said below
- noise_var: float32 [2], P('grp'), parts along dimension 0, may hold values from 0.5 to 2
Outputs:
- residual_out: float32 [4, 2048, 2048], P('grp', ('row', 'sub')), parts along dimension 0
- direction_out: float32 [4, 2048, 2048], P('grp', ('row', 'sub')), parts along dimension 0
- step_size: float32 [4], P('grp'), parts along dimension 0
There are 2 independent parts, one for each index of `grp`. A program takes and returns all parts, laid end to end along the dimension named above; each array names one. Nothing has to cross between parts.
Inputs may be any that keep to these rules, and one draw needn't show every extreme that they name: spectrum[k, l] = spectrum[(4096 - k) % 4096, (4096 - l) % 4096] for all k, l.
All inputs are finite; a program needn't handle non-finite values.
Results may differ from a plain program's by a relative error of at most 0.00005.
Values sent between devices are 32-bit elements; how exact they have to be, the bound alone decides.
A program may use at most 128 MiB of HBM per device.

v0:
```python
import functools
import math

import jax
import jax.numpy as jnp
import numpy as np
from jax import lax
from jax.experimental import pallas as pl
from jax.experimental.pallas import tpu as pltpu
from jax.sharding import PartitionSpec as P

LANES = 128
TINY = 1e-06
CHUNKS = 4
MESH = pl.DeviceIdType.MESH
GRANT = 60 * 1024 * 1024


def unit(turns, modulus, orient):
    angle = orient * 2.0 * np.pi * (np.asarray(turns) % modulus) / modulus
    return np.cos(angle), np.sin(angle)


def halves(table):
    table = np.asarray(table, np.float32)
    hi = table.astype(jnp.bfloat16)
    lo = (table - hi.astype(np.float32)).astype(jnp.bfloat16)
    return jnp.asarray(np.stack([hi, lo]))


def complex_block(cos_part, sin_part):
    return np.stack(
        [np.stack([cos_part, sin_part], 1), np.stack([-sin_part, cos_part], 1)], 0
    )


def split(x):
    hi = x.astype(jnp.bfloat16)
    return hi, (x - hi.astype(jnp.float32)).astype(jnp.bfloat16)


def dot(a, b):
    return jnp.dot(a, b, preferred_element_type=jnp.float32)


def dot_right(x, table_ref):
    hi, lo = split(x)
    return dot(hi, table_ref[0]) + (dot(lo, table_ref[0]) + dot(hi, table_ref[1]))


def dot_left(table_ref, x):
    hi, lo = split(x)
    return dot(table_ref[0], hi) + (dot(table_ref[0], lo) + dot(table_ref[1], hi))


def turn(z, k, n, orient):
    k = k % n
    re, im = z
    if k == 0:
        return z
    if 2 * k == n:
        return -re, -im
    if 4 * k == n or 4 * k == 3 * n:
        sign = orient if 4 * k == n else -orient
        return (-im, re) if sign > 0 else (im, -re)
    c = math.cos(2 * math.pi * k / n)
    s = orient * math.sin(2 * math.pi * k / n)
    return re * c - im * s, re * s + im * c


def add(u, v):
    return u[0] + v[0], u[1] + v[1]


def sub(u, v):
    return u[0] - v[0], u[1] - v[1]


def butterflies(xs, orient):
    n = len(xs)
    if n == 1:
        return xs
    even = butterflies(xs[0::2], orient)
    odd = butterflies(xs[1::2], orient)
    odd = [turn(z, k, n, orient) for k, z in enumerate(odd)]
    return [add(e, o) for e, o in zip(even, odd)] + [sub(e, o) for e, o in zip(even, odd)]


def padded_forward(xs):
    n = len(xs)
    even = butterflies(xs, -1)
    odd = butterflies([turn(z, a, 2 * n, -1) for a, z in enumerate(xs)], -1)
    return [even[i // 2] if i % 2 == 0 else odd[i // 2] for i in range(2 * n)]


def cut_inverse(zs):
    n = len(zs) // 2
    even = butterflies(zs[0::2], 1)
    odd = butterflies(zs[1::2], 1)
    return [add(even[a], turn(odd[a], a, 2 * n, 1)) for a in range(n)]


def rotate(re, im, c, s):
    return re * c - im * s, re * s + im * c


def row_kernel(low, groups, dir_ref, table_ref, cos_ref, sin_ref, *rest):
    outs, work, turned = rest[:-2], rest[-2], rest[-1]
    half = low // 2
    rows = dir_ref.shape[1]
    for c in range(2):
        for a in range(half):
            turned[a, c] = dir_ref[c, :, a * LANES : (a + 1) * LANES].T

    def spread(t, carry):
        at = pl.ds(pl.multiple_of(t * 8, 8), 8)
        xs = [(turned[a, 0, at, :], turned[a, 1, at, :]) for a in range(half)]
        cos_rows, sin_rows = cos_ref[at, :], sin_ref[at, :]
        for m, (re, im) in enumerate(padded_forward(xs)):
            re, im = rotate(re, im, cos_rows[:, m : m + 1], sin_rows[:, m : m + 1])
            work[m, 0, at, :] = re
            work[m, 1, at, :] = im
        return carry

    lax.fori_loop(0, LANES // 8, spread, 0)
    per_chunk = low // len(outs)
    for i, out in enumerate(outs):

        def column(m, carry):
            got = dot_left(table_ref, work[i * per_chunk + m].reshape(2 * LANES, rows))
            size = 2 * LANES // groups
            for j in range(groups):
                out[j, m] = got[j * size : (j + 1) * size]
            return carry

        lax.fori_loop(0, per_chunk, column, 0)


def column_kernel(low, per, x_ref, w_ref, fwd_ref, inv_ref, cos_ref, sin_ref, out_ref, work):
    half = low // 2
    count = x_ref.shape[1]

    def spread(m, carry):
        xs = [(x_ref[a, m, :per], x_ref[a, m, per:]) for a in range(half)]
        for k, (re, im) in enumerate(padded_forward(xs)):
            re, im = rotate(re, im, cos_ref[k : k + 1, :], sin_ref[k : k + 1, :])
            work[k, m, :, :LANES] = re
            work[k, m, :, LANES:] = im
        return carry

    lax.fori_loop(0, count, spread, 0)

    def filtered(k, carry):
        spectral = dot_right(work[k].reshape(count * per, 2 * LANES), fwd_ref)
        weights = w_ref[k].reshape(count * per, LANES)
        spectral = spectral * jnp.concatenate([weights, weights], axis=1)
        got = dot_right(spectral, inv_ref)
        cos_row, sin_row = cos_ref[pl.ds(k, 1), :], sin_ref[pl.ds(k, 1), :]
        re, im = rotate(got[:, :LANES], got[:, LANES:], cos_row, -sin_row)
        work[k, :, :, :LANES] = re.reshape(count, per, LANES)
        work[k, :, :, LANES:] = im.reshape(count, per, LANES)
        return carry

    lax.fori_loop(0, low, filtered, 0)

    def gather(m, carry):
        zs = [(work[k, m, :, :LANES], work[k, m, :, LANES:]) for k in range(low)]
        for a, (re, im) in enumerate(cut_inverse(zs)):
            out_ref[a, m, :per] = re
            out_ref[a, m, per:] = im
        return carry

    lax.fori_loop(0, count, gather, 0)


def image_kernel(low, groups, chunks, *refs):
    ins = refs[:chunks]
    dir_ref, res_ref, noise_ref, table_ref, cos_ref, sin_ref = refs[chunks : chunks + 6]
    image_ref, sums_ref, work, applied = refs[chunks + 6 :]
    half = low // 2
    rows = dir_ref.shape[1]
    per_chunk = low // chunks
    for i, x_ref in enumerate(ins):

        def column(m, carry):
            parts = [x_ref[j, m] for j in range(groups)]
            got = dot_left(table_ref, parts[0] if groups == 1 else jnp.concatenate(parts, axis=0))
            work[i * per_chunk + m] = got.reshape(2, LANES, rows)
            return carry

        lax.fori_loop(0, per_chunk, column, 0)

    def gather(t, carry):
        at = pl.ds(pl.multiple_of(t * 8, 8), 8)
        cos_rows, sin_rows = cos_ref[at, :], sin_ref[at, :]
        zs = []
        for m in range(low):
            zs.append(
                rotate(work[m, 0, at, :], work[m, 1, at, :], cos_rows[:, m : m + 1], -sin_rows[:, m : m + 1])
            )
        for a, (re, im) in enumerate(cut_inverse(zs)):
            applied[a, 0, at, :] = re
            applied[a, 1, at, :] = im
        return carry

    lax.fori_loop(0, LANES // 8, gather, 0)
    noise = noise_ref[0]
    for c in range(2):
        totals = [jnp.zeros((rows, LANES), jnp.float32)] * 4
        for a in range(half):
            cols = slice(a * LANES, (a + 1) * LANES)
            d, r = dir_ref[c, :, cols], res_ref[c, :, cols]
            image = applied[a, c].T + noise * d
            image_ref[c, :, cols] = image
            for s, term in enumerate((r * r, d * image, r * image, image * image)):
                totals[s] = totals[s] + term
        for s in range(4):
            sums_ref[4 * c + s : 4 * c + s + 1, :] = jnp.sum(totals[s], axis=0, keepdims=True)


def update_kernel(n_row, n_sub, sums_ref, image_ref, dir_ref, res_ref, r_out, d_out, s_out, held, send_sem, recv_sem):
    n = n_row * n_sub
    me = lax.axis_index("row") * n_sub + lax.axis_index("sub")

    def place(o):
        peer = lax.rem(me + o, n)
        return {"row": peer // n_sub, "sub": lax.rem(peer, n_sub)}

    barrier = pltpu.get_barrier_semaphore()

    def greet(o, carry):
        pl.semaphore_signal(barrier, inc=1, device_id=place(o), device_id_type=MESH)
        return carry

    lax.fori_loop(1, n, greet, 0)
    pl.semaphore_wait(barrier, n - 1)

    def copy(o):
        return pltpu.make_async_remote_copy(
            src_ref=sums_ref,
            dst_ref=held.at[me],
            send_sem=send_sem.at[o],
            recv_sem=recv_sem.at[o],
            device_id=place(o),
            device_id_type=MESH,
        )

    def start(o, carry):
        copy(o).start()
        return carry

    lax.fori_loop(1, n, start, 0)
    held[me] = sums_ref[...]

    def finish(o, carry):
        copy(o).wait()
        return carry

    lax.fori_loop(1, n, finish, 0)
    total = jnp.sum(jnp.sum(held[...], axis=0), axis=1, keepdims=True)
    for c in range(2):
        old, curve, cross, square = [total[4 * c + s : 4 * c + s + 1] for s in range(4)]
        step = old / curve
        new = jnp.maximum(old - 2.0 * step * cross + step * step * square, 0.0)
        beta = new / (old + TINY)
        s_out[c : c + 1, :] = jnp.broadcast_to(step, (1, LANES))
        rows = min(8, res_ref.shape[1])

        def strip(t, carry):
            at = pl.ds(pl.multiple_of(t * rows, rows), rows)
            r = res_ref[c, at, :] - step * image_ref[c, at, :]
            r_out[c, at, :] = r
            d_out[c, at, :] = r + beta * dir_ref[c, at, :]
            return carry

        lax.fori_loop(0, res_ref.shape[1] // rows, strip, 0)


def params(**more):
    return pltpu.CompilerParams(vmem_limit_bytes=GRANT, **more)


def make_tables(embed, n, per):
    low, f32 = embed // LANES, jnp.float32
    slots, seconds = np.arange(LANES), np.arange(low)
    turn_cos, turn_sin = unit(slots[:, None] * seconds[None, :], embed, -1.0)
    wide_cos, wide_sin = jnp.asarray(turn_cos, f32), jnp.asarray(turn_sin, f32)
    tall_cos, tall_sin = jnp.asarray(turn_cos.T, f32), jnp.asarray(turn_sin.T, f32)
    fwd = complex_block(*unit(slots[:, None] * slots[None, :], LANES, -1.0))
    inv = complex_block(*unit(slots[:, None] * slots[None, :], LANES, 1.0))
    scale = 1.0 / (embed * embed)
    col_fwd = halves(fwd.reshape(2 * LANES, 2 * LANES))
    col_inv = halves(inv.reshape(2 * LANES, 2 * LANES) * scale)
    row_fwd = halves(
        fwd.reshape(2, LANES, 2, n, per).transpose(3, 2, 4, 0, 1).reshape(2 * LANES, 2 * LANES)
    )
    row_inv = halves(
        inv.reshape(2, n, per, 2, LANES).transpose(3, 4, 1, 0, 2).reshape(2 * LANES, 2 * LANES)
    )
    return row_fwd, row_inv, col_fwd, col_inv, wide_cos, wide_sin, tall_cos, tall_sin


def pair_body(n_row, n_sub, residual_in, direction, weights, noise_var):
    _, rows, grid_len = direction.shape
    embed = 2 * grid_len
    low, half = embed // LANES, grid_len // LANES
    n = n_row * n_sub
    per = LANES // n
    f32 = jnp.float32
    vmem = pl.BlockSpec(memory_space=pltpu.VMEM)
    chunks = CHUNKS
    per_chunk = low // chunks
    aligned = (2 * per) % 8 == 0
    groups = n if aligned else 1

    row_fwd, row_inv, col_fwd, col_inv, wide_cos, wide_sin, tall_cos, tall_sin = make_tables(embed, n, per)

    spread = pl.pallas_call(
        functools.partial(row_kernel, low, groups),
        out_shape=[jax.ShapeDtypeStruct((groups, per_chunk, 2 * LANES // groups, rows), f32)] * chunks,
        in_specs=[vmem] * 4,
        out_specs=[vmem] * chunks,
        scratch_shapes=[pltpu.VMEM((low, 2, LANES, rows), f32), pltpu.VMEM((half, 2, LANES, rows), f32)],
        compiler_params=params(),
        name="rows_out",
    )(direction, row_fwd, wide_cos, wide_sin)

    def swap(x):
        return lax.all_to_all(x, ("row", "sub"), split_axis=0, concat_axis=0, tiled=True)

    back = []
    for i, x in enumerate(spread):
        if not aligned:
            x = x.reshape(per_chunk, n, 2 * per, rows).transpose(1, 0, 2, 3)
        x = swap(x)
        if rows != LANES:
            x = x.reshape(half, LANES // rows, per_chunk, 2 * per, rows).transpose(0, 2, 3, 1, 4)
            x = x.reshape(half, per_chunk, 2 * per, LANES)
        x = pl.pallas_call(
            functools.partial(column_kernel, low, per),
            out_shape=jax.ShapeDtypeStruct((half, per_chunk, 2 * per, LANES), f32),
            in_specs=[vmem] * 6,
            out_specs=vmem,
            scratch_shapes=[pltpu.VMEM((low, per_chunk, per, 2 * LANES), f32)],
            compiler_params=params(),
            name=f"columns{i}",
        )(x, weights[:, i * per_chunk : (i + 1) * per_chunk], col_fwd, col_inv, tall_cos, tall_sin)
        if rows != LANES:
            x = x.reshape(half, per_chunk, 2 * per, LANES // rows, rows).transpose(0, 3, 1, 2, 4)
            x = x.reshape(n, per_chunk, 2 * per, rows)
        x = swap(x)
        if not aligned:
            x = x.transpose(1, 0, 2, 3).reshape(1, per_chunk, 2 * LANES, rows)
        back.append(x)

    image, sums = pl.pallas_call(
        functools.partial(image_kernel, low, groups, chunks),
        out_shape=[jax.ShapeDtypeStruct(direction.shape, f32), jax.ShapeDtypeStruct((8, LANES), f32)],
        in_specs=[vmem] * (chunks + 2) + [pl.BlockSpec(memory_space=pltpu.SMEM)] + [vmem] * 3,
        out_specs=[vmem] * 2,
        scratch_shapes=[pltpu.VMEM((low, 2, LANES, rows), f32), pltpu.VMEM((half, 2, LANES, rows), f32)],
        compiler_params=params(),
        name="rows_back",
    )(*back, direction, residual_in, noise_var, row_inv, wide_cos, wide_sin)

    residual_out, direction_out, steps = pl.pallas_call(
        functools.partial(update_kernel, n_row, n_sub),
        out_shape=[
            jax.ShapeDtypeStruct(direction.shape, f32),
            jax.ShapeDtypeStruct(direction.shape, f32),
            jax.ShapeDtypeStruct((2, LANES), f32),
        ],
        in_specs=[vmem] * 4,
        out_specs=[vmem] * 3,
        scratch_shapes=[
            pltpu.VMEM((n, 8, LANES), f32),
            pltpu.SemaphoreType.DMA((n,)),
            pltpu.SemaphoreType.DMA((n,)),
        ],
        compiler_params=params(collective_id=0, has_side_effects=True),
        name="update",
    )(sums, image, direction, residual_in)
    return residual_out, direction_out, steps[:, 0]


def fused_kernel(
    low, chunks, n_row, n_sub,
    dir_ref, res_hbm, spec_hbm, noise_ref, row_fwd, row_inv, col_fwd, col_inv,
    wide_cos, wide_sin, tall_cos, tall_sin,
    r_out, d_out, s_out,
    res_ref, spec_ref, weights, work, turned, cols, send, recv, back_send, back_recv, held, sums_ref,
    load_sem, send_sem, recv_sem, back_send_sem, back_recv_sem, sum_send_sem, sum_recv_sem,
):
    n = n_row * n_sub
    half = low // 2
    count = low // chunks
    per = LANES // n
    size = 2 * per
    me = lax.axis_index("row") * n_sub + lax.axis_index("sub")

    def place(o):
        peer = lax.rem(me + o, n)
        return peer, {"row": peer // n_sub, "sub": lax.rem(peer, n_sub)}

    def loop(first, last, step):
        def run(i, carry):
            step(i)
            return carry

        lax.fori_loop(first, last, run, 0)

    barrier = pltpu.get_barrier_semaphore()
    loop(
        1, n,
        lambda o: pl.semaphore_signal(barrier, inc=1, device_id=place(o)[1], device_id_type=MESH),
    )
    load_res = pltpu.make_async_copy(res_hbm, res_ref, load_sem.at[0])
    load_spec = [
        pltpu.make_async_copy(spec_hbm.at[:, pl.ds(s * LANES, LANES)], spec_ref.at[s], load_sem.at[s + 1])
        for s in range(spec_ref.shape[0])
    ]
    for load in load_spec:
        load.start()
    load_res.start()

    def exchange(i, o, src, dst, s_sem, r_sem):
        peer, device = place(o)
        return pltpu.make_async_remote_copy(
            src_ref=src.at[i, peer],
            dst_ref=dst.at[i, me],
            send_sem=s_sem.at[i, o],
            recv_sem=r_sem.at[i, o],
            device_id=device,
            device_id_type=MESH,
        )

    def ahead(i, o):
        return exchange(i, o, send, recv, send_sem, recv_sem)

    def home(i, o):
        return exchange(i, o, back_send, back_recv, back_send_sem, back_recv_sem)

    for c in range(2):
        for a in range(half):
            turned[a, c] = dir_ref[c, :, a * LANES : (a + 1) * LANES].T

    def spread_rows(t):
        at = pl.ds(pl.multiple_of(t * 8, 8), 8)
        xs = [(turned[a, 0, at, :], turned[a, 1, at, :]) for a in range(half)]
        cos_rows, sin_rows = wide_cos[at, :], wide_sin[at, :]
        for m, (re, im) in enumerate(padded_forward(xs)):
            re, im = rotate(re, im, cos_rows[:, m : m + 1], sin_rows[:, m : m + 1])
            work[m, 0, at, :] = re
            work[m, 1, at, :] = im

    loop(0, LANES // 8, spread_rows)

    def send_chunk(i):
        def column(m):
            got = dot_left(row_fwd, work[i * count + m].reshape(2 * LANES, LANES))
            for j in range(n):
                send[i, j, m] = got[j * size : (j + 1) * size]

        loop(0, count, column)
        recv[i, me] = send[i, me]
        loop(1, n, lambda o: ahead(i, o).start())

    for i in range(chunks):
        if i == 0:
            pl.semaphore_wait(barrier, n - 1)
        send_chunk(i)

    for load in load_spec:
        load.wait()

    def turn_spectrum(k):
        for s in range(spec_ref.shape[0]):
            part = spec_ref[s, pl.ds(k, LANES, stride=low), :]
            weights[k, s * LANES : (s + 1) * LANES, :] = part.T

    loop(0, low, turn_spectrum)

    def column_chunk(i):
        loop(1, n, lambda o: ahead(i, o).wait_recv())

        def spread(m):
            xs = [(recv[i, a, m, :per], recv[i, a, m, per:]) for a in range(half)]
            for k, (re, im) in enumerate(padded_forward(xs)):
                re, im = rotate(re, im, tall_cos[k : k + 1, :], tall_sin[k : k + 1, :])
                cols[k, m, :, :LANES] = re
                cols[k, m, :, LANES:] = im

        loop(0, count, spread)

        def filtered(k):
            spectral = dot_right(cols[k].reshape(count * per, 2 * LANES), col_fwd)
            scale = jnp.concatenate(
                [weights[k, pl.ds(i * count + m, per, stride=low), :] for m in range(count)], axis=0
            )
            spectral = spectral * jnp.concatenate([scale, scale], axis=1)
            got = dot_right(spectral, col_inv)
            cos_row, sin_row = tall_cos[pl.ds(k, 1), :], tall_sin[pl.ds(k, 1), :]
            re, im = rotate(got[:, :LANES], got[:, LANES:], cos_row, -sin_row)
            cols[k, :, :, :LANES] = re.reshape(count, per, LANES)
            cols[k, :, :, LANES:] = im.reshape(count, per, LANES)

        loop(0, low, filtered)

        def gather(m):
            zs = [(cols[k, m, :, :LANES], cols[k, m, :, LANES:]) for k in range(low)]
            for a, (re, im) in enumerate(cut_inverse(zs)):
                back_send[i, a, m, :per] = re
                back_send[i, a, m, per:] = im

        loop(0, count, gather)
        back_recv[i, me] = back_send[i, me]
        loop(1, n, lambda o: home(i, o).start())

    for i in range(chunks):
        column_chunk(i)

    for i in range(chunks):
        loop(1, n, lambda o: home(i, o).wait_recv())

        def column(m):
            got = dot_left(row_inv, jnp.concatenate([back_recv[i, j, m] for j in range(n)], axis=0))
            work[i * count + m] = got.reshape(2, LANES, LANES)

        loop(0, count, column)

    def gather_rows(t):
        at = pl.ds(pl.multiple_of(t * 8, 8), 8)
        cos_rows, sin_rows = wide_cos[at, :], wide_sin[at, :]
        zs = [
            rotate(work[m, 0, at, :], work[m, 1, at, :], cos_rows[:, m : m + 1], -sin_rows[:, m : m + 1])
            for m in range(low)
        ]
        for a, (re, im) in enumerate(cut_inverse(zs)):
            turned[a, 0, at, :] = re
            turned[a, 1, at, :] = im

    loop(0, LANES // 8, gather_rows)
    load_res.wait()
    noise = noise_ref[0]
    for c in range(2):
        totals = [jnp.zeros((8, LANES), jnp.float32)] * 4
        for a in range(half):
            at = slice(a * LANES, (a + 1) * LANES)
            d, r = dir_ref[c, :, at], res_ref[c, :, at]
            image = turned[a, c].T + noise * d
            d_out[c, :, at] = image
            for s, term in enumerate((r * r, d * image, r * image, image * image)):
                totals[s] = totals[s] + jnp.sum(term.reshape(LANES // 8, 8, LANES), axis=0)
        for s in range(4):
            sums_ref[4 * c + s : 4 * c + s + 1, :] = jnp.sum(totals[s], axis=0, keepdims=True)

    def share(o):
        return pltpu.make_async_remote_copy(
            src_ref=sums_ref,
            dst_ref=held.at[me],
            send_sem=sum_send_sem.at[o],
            recv_sem=sum_recv_sem.at[o],
            device_id=place(o)[1],
            device_id_type=MESH,
        )

    held[me] = sums_ref[...]
    loop(1, n, lambda o: share(o).start())
    for i in range(chunks):
        loop(1, n, lambda o: ahead(i, o).wait_send())
        loop(1, n, lambda o: home(i, o).wait_send())
    loop(1, n, lambda o: share(o).wait())
    total = jnp.sum(jnp.sum(held[...], axis=0), axis=1, keepdims=True)
    for c in range(2):
        old, curve, cross, square = [total[4 * c + s : 4 * c + s + 1] for s in range(4)]
        step = old / curve
        new = jnp.maximum(old - 2.0 * step * cross + step * step * square, 0.0)
        beta = new / (old + TINY)
        s_out[c : c + 1, :] = jnp.broadcast_to(step, (1, LANES))

        def strip(t):
            at = pl.ds(pl.multiple_of(t * 8, 8), 8)
            r = res_ref[c, at, :] - step * d_out[c, at, :]
            r_out[c, at, :] = r
            d_out[c, at, :] = r + beta * dir_ref[c, at, :]

        loop(0, LANES // 8, strip)


def fused_body(n_row, n_sub, residual_in, direction, spectrum, noise_var):
    _, rows, grid_len = direction.shape
    embed = 2 * grid_len
    low, half = embed // LANES, grid_len // LANES
    n = n_row * n_sub
    per = LANES // n
    f32 = jnp.float32
    vmem = pl.BlockSpec(memory_space=pltpu.VMEM)
    away = pl.BlockSpec(memory_space=pl.ANY)
    chunks = CHUNKS
    count = low // chunks
    tables = make_tables(embed, n, per)
    block = pltpu.VMEM((chunks, n, count, 2 * per, LANES), f32)
    flags = pltpu.SemaphoreType.DMA((chunks, n))
    residual_out, direction_out, steps = pl.pallas_call(
        functools.partial(fused_kernel, low, chunks, n_row, n_sub),
        out_shape=[
            jax.ShapeDtypeStruct(direction.shape, f32),
            jax.ShapeDtypeStruct(direction.shape, f32),
            jax.ShapeDtypeStruct((2, LANES), f32),
        ],
        in_specs=[vmem, away, away, pl.BlockSpec(memory_space=pltpu.SMEM)] + [vmem] * 8,
        out_specs=[vmem] * 3,
        scratch_shapes=[
            pltpu.VMEM(direction.shape, f32),
            pltpu.VMEM((spectrum.shape[1] // LANES, embed, LANES), f32),
            pltpu.VMEM((low, spectrum.shape[1], LANES), f32),
            pltpu.VMEM((low, 2, LANES, rows), f32),
            pltpu.VMEM((half, 2, LANES, rows), f32),
            pltpu.VMEM((low, count, per, 2 * LANES), f32),
            block, block, block, block,
            pltpu.VMEM((n, 8, LANES), f32),
            pltpu.VMEM((8, LANES), f32),
            pltpu.SemaphoreType.DMA((1 + spectrum.shape[1] // LANES,)),
            flags, flags, flags, flags,
            pltpu.SemaphoreType.DMA((n,)),
            pltpu.SemaphoreType.DMA((n,)),
        ],
        compiler_params=params(collective_id=1, has_side_effects=True),
        name="cg_step",
    )(direction, residual_in, spectrum, noise_var, *tables)
    return residual_out, direction_out, steps[:, 0]


def solution(mesh):
    n_row, n_sub = mesh.shape["row"], mesh.shape["sub"]

    def body(residual_in, direction, spectrum, noise_var):
        embed = spectrum.shape[0]
        low = embed // LANES
        per = LANES // (n_row * n_sub)
        if direction.shape[1] == LANES and direction.shape[2] == LANES * n_row * n_sub and per % 8 == 0:
            return fused_body(n_row, n_sub, residual_in, direction, spectrum, noise_var)
        weights = spectrum.reshape(LANES, low, per, low).transpose(1, 3, 2, 0)
        return pair_body(n_row, n_sub, residual_in, direction, weights, noise_var)

    placed = P("grp", ("row", "sub"), None)
    return jax.shard_map(
        body,
        mesh=mesh,
        in_specs=(placed, placed, P("grp", ("row", "sub")), P("grp")),
        out_specs=(placed, placed, P("grp")),
        check_vma=False,
    )
```

profile of v0, /device:TPU:0, one launch (start us, length us, event | category | flops | bytes accessed | tf_op | source)
XLA Modules:
  0.0 215.2 jit_solution(3315147192537206939)
XLA Ops:
  1.3 208.0 %cg_step.1 = (f32[2,128,2048]{2,1,0:T(8,128)}, f32[2,128,2048]{2,1,0:T(8,128)}, f32[2,128]{1,0:T(2,128)}) custom-call(f32[2,128,2048]{2,1,0:T(8,128)} %dir_ref.1, f32[2,128,2048]{2,1,0:T(8,128)} %res_hbm.1, f32[4096,256]{1,0:T(8,128)} %spec_hbm.1, f32[1]{0:T(128)S(6)} %copy.17.noise_ref, bf16[2,256,256]{2,1,0:T(8,128)(2,1)} %constant.22.clone.row_fwd, ...), custom_call_target="tpu_custom_call" | custom-call | tf_op jit(solution)/shard_map/cg_step/pallas_call | solution.py:604
  209.3 1.3 slice_reduce_fusion
  210.5 0.0 copy-start
  210.5 3.3 %copy.18 = f32[2,128,2048]{2,1,0:T(8,128)} copy(f32[2,128,2048]{2,1,0:T(8,128)} %get-tuple-element.12) | data formatting | bytes 4194304
  213.8 0.0 copy-done
  213.8 1.3 copy.19
Async XLA Ops:
  210.5 3.3 %copy-start = (f32[2,128,2048]{2,1,0:T(8,128)S(1)}, f32[2,128,2048]{2,1,0:T(8,128)}, u32[]{:S(2)}) copy-start(f32[2,128,2048]{2,1,0:T(8,128)} %get-tuple-element.13) | copy-start | bytes 6291460
where the time goes:
time: 215 us
  Pallas kernels  208 us (97%)
  local copies, waits for them, and re-layouts  5.89 us (3%)
    pallas_call x1, Pallas kernels, fused_body(): pl.pallas_call(functools.partial(fused_kernel, low, chunks, n_row, n_sub)...  208 us
    unnamed x4, local copies, waits for them, and re-layouts  4.61 us

commit v1 on v0

--- a/solution.py
+++ b/solution.py
@@ -12,6 +12,7 @@
 LANES = 128
 TINY = 1e-06
 CHUNKS = 4
+PIECES = 4
 MESH = pl.DeviceIdType.MESH
 GRANT = 60 * 1024 * 1024
 
@@ -383,92 +384,201 @@
     return residual_out, direction_out, steps[:, 0]
 
 
-def fused_kernel(
-    low, chunks, n_row, n_sub,
-    dir_ref, res_hbm, spec_hbm, noise_ref, row_fwd, row_inv, col_fwd, col_inv,
-    wide_cos, wide_sin, tall_cos, tall_sin,
+def odd_terms(d, n):
+    q = n // 4
+    zs = butterflies([turn((d[a], -d[a + q]), a, n, -1) for a in range(q)], -1)
+    return {4 * j + 1: z for j, z in enumerate(zs)}
+
+
+def real_forward(xs):
+    n = len(xs)
+    if n == 1:
+        return {0: (xs[0], None)}
+    if n == 2:
+        return {0: (xs[0] + xs[1], None), 1: (xs[0] - xs[1], None)}
+    h = n // 2
+    out = {2 * k: z for k, z in real_forward([xs[a] + xs[a + h] for a in range(h)]).items()}
+    out.update(odd_terms([xs[a] - xs[a + h] for a in range(h)], n))
+    return out
+
+
+def real_padded(xs):
+    n = 2 * len(xs)
+    out = {2 * k: z for k, z in real_forward(xs).items()}
+    out.update(odd_terms(xs, n))
+    return out
+
+
+def odd_values(pairs, n):
+    q = n // 4
+    zs = [turn(z, a, n, 1) for a, z in enumerate(butterflies([pairs[4 * j + 1] for j in range(q)], 1))]
+    return [z[0] for z in zs] + [-z[1] for z in zs]
+
+
+def real_inverse(pairs, n):
+    if n == 1:
+        return [pairs[0][0]]
+    if n == 2:
+        return [pairs[0][0] + pairs[1][0], pairs[0][0] - pairs[1][0]]
+    even = real_inverse({k // 2: z for k, z in pairs.items() if k % 2 == 0}, n // 2)
+    odd = odd_values(pairs, n)
+    return [e + o for e, o in zip(even, odd)] + [e - o for e, o in zip(even, odd)]
+
+
+def real_cut(pairs, n):
+    even = real_inverse({k // 2: z for k, z in pairs.items() if k % 2 == 0}, n // 2)
+    return [e + o for e, o in zip(even, odd_values(pairs, n))]
+
+
+def real_names(n):
+    if n <= 2:
+        return list(range(n))
+    return [2 * k for k in real_names(n // 2)] + list(range(1, n, 4))
+
+
+def loop(first, last, step):
+    def run(i, carry):
+        step(i)
+        return carry
+
+    lax.fori_loop(first, last, run, 0)
+
+
+def half_kernel(
+    low, chunks, pieces, n_row, n_sub,
+    dir_ref, res_hbm, spec_hbm, noise_ref, row_fwd, row_inv, col_fwd, col_inv, tall_cos, tall_sin,
     r_out, d_out, s_out,
-    res_ref, spec_ref, weights, work, turned, cols, send, recv, back_send, back_recv, held, sums_ref,
-    load_sem, send_sem, recv_sem, back_send_sem, back_recv_sem, sum_send_sem, sum_recv_sem,
+    res_ref, spec_ref, weights, work, cols, send, recv, back_send, back_recv,
+    raw_in, img_send, img_in, x_send, x_recv, xb_send, xb_recv, held, sums_ref,
+    load_sem, raw_ssem, raw_rsem, img_ssem, img_rsem, send_sem, recv_sem, back_ssem, back_rsem,
+    x_ssem, x_rsem, xb_ssem, xb_rsem, sum_ssem, sum_rsem,
 ):
     n = n_row * n_sub
+    hs = n_sub // 2
+    g = n_row * hs
     half = low // 2
     count = low // chunks
     per = LANES // n
     size = 2 * per
-    me = lax.axis_index("row") * n_sub + lax.axis_index("sub")
+    step_rows = LANES // pieces
+    my_r, my_s = lax.axis_index("row"), lax.axis_index("sub")
+    h = my_s // hs
+    gi = my_r * hs + lax.rem(my_s, hs)
+    me = my_r * n_sub + my_s
+    mate_s = n_sub - 1 - my_s
+    mate = {"row": my_r, "sub": mate_s}
+    slabs = [me, my_r * n_sub + mate_s]
+    lead = my_s == h * hs
 
     def place(o):
         peer = lax.rem(me + o, n)
-        return peer, {"row": peer // n_sub, "sub": lax.rem(peer, n_sub)}
-
-    def loop(first, last, step):
-        def run(i, carry):
-            step(i)
-            return carry
-
-        lax.fori_loop(first, last, run, 0)
+        return {"row": peer // n_sub, "sub": lax.rem(peer, n_sub)}
+
+    def ally(d, part):
+        r, s = d // hs, part * hs + lax.rem(d, hs)
+        return {"row": r, "sub": s}, [r * n_sub + s, r * n_sub + n_sub - 1 - s]
+
+    def leader(e):
+        return {"row": e, "sub": (1 - h) * hs}
 
     barrier = pltpu.get_barrier_semaphore()
     loop(
         1, n,
-        lambda o: pl.semaphore_signal(barrier, inc=1, device_id=place(o)[1], device_id_type=MESH),
+        lambda o: pl.semaphore_signal(barrier, inc=1, device_id=place(o), device_id_type=MESH),
     )
     load_res = pltpu.make_async_copy(res_hbm, res_ref, load_sem.at[0])
     load_spec = [
         pltpu.make_async_copy(spec_hbm.at[:, pl.ds(s * LANES, LANES)], spec_ref.at[s], load_sem.at[s + 1])
         for s in range(spec_ref.shape[0])
     ]
+
+    def remote(src, dst, s_sem, r_sem, device):
+        return pltpu.make_async_remote_copy(
+            src_ref=src, dst_ref=dst, send_sem=s_sem, recv_sem=r_sem, device_id=device, device_id_type=MESH
+        )
+
+    def raw_copy(p):
+        at = pl.ds(pl.multiple_of(p * step_rows, step_rows), step_rows)
+        return remote(dir_ref.at[1 - h, at, :], raw_in.at[at, :], raw_ssem.at[p], raw_rsem.at[p], mate)
+
+    def img_copy(p):
+        at = pl.ds(pl.multiple_of(p * step_rows, step_rows), step_rows)
+        return remote(img_send.at[at, :], img_in.at[at, :], img_ssem.at[p], img_rsem.at[p], mate)
+
+    def ahead(i, b, o):
+        p = lax.rem(gi + o, g)
+        return remote(
+            send.at[i, b, p], recv.at[i, slabs[b]], send_sem.at[i, b, o], recv_sem.at[i, b, o], ally(p, h)[0]
+        )
+
+    def home(i, b, o):
+        p = lax.rem(gi + o, g)
+        device, places = ally(p, h)
+        return remote(
+            back_send.at[i, places[b]], back_recv.at[i, b, gi], back_ssem.at[i, b, o], back_rsem.at[i, b, o], device
+        )
+
+    def x_ahead(e):
+        return remote(x_send.at[e], x_recv.at[gi], x_ssem.at[e], x_rsem.at[gi], leader(e))
+
+    def x_arrival(d):
+        return remote(x_send.at[0], x_recv.at[d], x_ssem.at[0], x_rsem.at[d], mate)
+
+    def x_home(d):
+        return remote(xb_send.at[d], xb_recv.at[my_r], xb_ssem.at[d], xb_rsem.at[my_r], ally(d, 1 - h)[0])
+
+    def x_back(e):
+        return remote(xb_send.at[0], xb_recv.at[e], xb_ssem.at[0], xb_rsem.at[e], mate)
+
+    pl.semaphore_wait(barrier, n - 1)
+    loop(0, pieces, lambda p: raw_copy(p).start())
     for load in load_spec:
         load.start()
     load_res.start()
 
-    def exchange(i, o, src, dst, s_sem, r_sem):
-        peer, device = place(o)
-        return pltpu.make_async_remote_copy(
-            src_ref=src.at[i, peer],
-            dst_ref=dst.at[i, me],
-            send_sem=s_sem.at[i, o],
-            recv_sem=r_sem.at[i, o],
-            device_id=device,
-            device_id_type=MESH,
-        )
-
-    def ahead(i, o):
-        return exchange(i, o, send, recv, send_sem, recv_sem)
-
-    def home(i, o):
-        return exchange(i, o, back_send, back_recv, back_send_sem, back_recv_sem)
-
-    for c in range(2):
-        for a in range(half):
-            turned[a, c] = dir_ref[c, :, a * LANES : (a + 1) * LANES].T
-
-    def spread_rows(t):
+    def row_strip(read, t):
         at = pl.ds(pl.multiple_of(t * 8, 8), 8)
-        xs = [(turned[a, 0, at, :], turned[a, 1, at, :]) for a in range(half)]
-        cos_rows, sin_rows = wide_cos[at, :], wide_sin[at, :]
-        for m, (re, im) in enumerate(padded_forward(xs)):
-            re, im = rotate(re, im, cos_rows[:, m : m + 1], sin_rows[:, m : m + 1])
-            work[m, 0, at, :] = re
-            work[m, 1, at, :] = im
-
-    loop(0, LANES // 8, spread_rows)
-
-    def send_chunk(i):
-        def column(m):
-            got = dot_left(row_fwd, work[i * count + m].reshape(2 * LANES, LANES))
-            for j in range(n):
-                send[i, j, m] = got[j * size : (j + 1) * size]
-
-        loop(0, count, column)
-        recv[i, me] = send[i, me]
-        loop(1, n, lambda o: ahead(i, o).start())
-
-    for i in range(chunks):
-        if i == 0:
-            pl.semaphore_wait(barrier, n - 1)
-        send_chunk(i)
+        found = real_padded([read(at, slice(a * LANES, (a + 1) * LANES)) for a in range(half)])
+        for m in range(low):
+            c, s = tall_cos[m : m + 1, :], tall_sin[m : m + 1, :]
+            re, im = found[m] if m in found else found[low - m]
+            if im is None:
+                re, im = re * c, re * s
+            elif m in found:
+                re, im = rotate(re, im, c, s)
+            else:
+                re, im = re * c + im * s, re * s - im * c
+            work[m, at, :LANES] = re
+            work[m, at, LANES:] = im
+
+    batch = min(4, count)
+
+    def row_dots(x, table, at):
+        hi, lo = split(x)
+        return dot(hi, table[h, 0, :, at]) + (dot(lo, table[h, 0, :, at]) + dot(hi, table[h, 1, :, at]))
+
+    def row_extras(b):
+        got = row_dots(work[0], row_fwd, slice(LANES, 2 * LANES)).T
+        for e in range(n_row):
+            x_send[e, 2 * b : 2 * b + 2, :] = got[2 * e : 2 * e + 2]
+
+    def send_chunk(i, b):
+        def columns(t):
+            m = t * batch
+            x = work[pl.ds(i * count + m, batch)].reshape(batch * LANES, 2 * LANES)
+            got = row_dots(x, row_fwd, slice(0, LANES))
+            for k in range(batch):
+                part = got[k * LANES : (k + 1) * LANES].T
+                for d in range(g):
+                    send[i, b, d, m + k] = part[d * size : (d + 1) * size]
+
+        loop(0, count // batch, columns)
+        recv[i, slabs[b]] = send[i, b, gi]
+        loop(1, g, lambda o: ahead(i, b, o).start())
+
+    loop(0, LANES // 8, lambda t: row_strip(lambda at, cs: dir_ref[h, at, cs], t))
+    row_extras(0)
+    loop(0, chunks, lambda i: send_chunk(i, 0))
 
     for load in load_spec:
         load.wait()
@@ -480,8 +590,47 @@
 
     loop(0, low, turn_spectrum)
 
+    def raw_piece(p):
+        raw_copy(p).wait_recv()
+        loop(
+            p * (step_rows // 8), (p + 1) * (step_rows // 8),
+            lambda t: row_strip(lambda at, cs: raw_in[at, cs], t),
+        )
+
+    loop(0, pieces, raw_piece)
+    row_extras(1)
+    loop(0, n_row, lambda e: x_ahead(e).start())
+    loop(0, chunks, lambda i: send_chunk(i, 1))
+
+    wide = 8
+
+    def fix_in():
+        def one(d):
+            x_arrival(d).wait_recv()
+            for b, place_in in enumerate(ally(d, 1 - h)[1]):
+                re, im = x_recv[d, 2 * b : 2 * b + 1, :], x_recv[d, 2 * b + 1 : 2 * b + 2, :]
+                recv[0, place_in, 0, 0:1, :] = recv[0, place_in, 0, 0:1, :] - im
+                recv[0, place_in, 0, per : per + 1, :] = recv[0, place_in, 0, per : per + 1, :] + re
+
+        loop(0, g, one)
+
+    def fix_out():
+        def one(d):
+            for b, place_in in enumerate(ally(d, 1 - h)[1]):
+                re = 0.5 * back_send[0, place_in, 0, 0:1, :]
+                im = 0.5 * back_send[0, place_in, 0, per : per + 1, :]
+                back_send[0, place_in, 0, 0:1, :] = re
+                back_send[0, place_in, 0, per : per + 1, :] = im
+                xb_send[d, 2 * b : 2 * b + 1, :] = im
+                xb_send[d, 2 * b + 1 : 2 * b + 2, :] = -re
+            x_home(d).start()
+
+        loop(0, g, one)
+
     def column_chunk(i):
-        loop(1, n, lambda o: ahead(i, o).wait_recv())
+        for b in range(2):
+            loop(1, g, lambda o: ahead(i, b, o).wait_recv())
+        pl.when(jnp.logical_and(i == 0, lead))(fix_in)
 
         def spread(m):
             xs = [(recv[i, a, m, :per], recv[i, a, m, per:]) for a in range(half)]
@@ -491,20 +640,29 @@
                 cols[k, m, :, LANES:] = im
 
         loop(0, count, spread)
-
-        def filtered(k):
-            spectral = dot_right(cols[k].reshape(count * per, 2 * LANES), col_fwd)
+        block = count * per
+
+        def filtered(t):
+            k = t * wide
+            spectral = dot_right(cols[pl.ds(k, wide)].reshape(wide * block, 2 * LANES), col_fwd)
             scale = jnp.concatenate(
-                [weights[k, pl.ds(i * count + m, per, stride=low), :] for m in range(count)], axis=0
+                [
+                    weights[k + w, pl.ds(i * count + m, per, stride=low), :]
+                    for w in range(wide)
+                    for m in range(count)
+                ],
+                axis=0,
             )
             spectral = spectral * jnp.concatenate([scale, scale], axis=1)
             got = dot_right(spectral, col_inv)
-            cos_row, sin_row = tall_cos[pl.ds(k, 1), :], tall_sin[pl.ds(k, 1), :]
-            re, im = rotate(got[:, :LANES], got[:, LANES:], cos_row, -sin_row)
-            cols[k, :, :, :LANES] = re.reshape(count, per, LANES)
-            cols[k, :, :, LANES:] = im.reshape(count, per, LANES)
-
-        loop(0, low, filtered)
+            for w in range(wide):
+                cos_row, sin_row = tall_cos[pl.ds(k + w, 1), :], tall_sin[pl.ds(k + w, 1), :]
+                part = got[w * block : (w + 1) * block]
+                re, im = rotate(part[:, :LANES], part[:, LANES:], cos_row, -sin_row)
+                cols[k + w, :, :, :LANES] = re.reshape(count, per, LANES)
+                cols[k + w, :, :, LANES:] = im.reshape(count, per, LANES)
+
+        loop(0, low // wide, filtered)
 
         def gather(m):
             zs = [(cols[k, m, :, :LANES], cols[k, m, :, LANES:]) for k in range(low)]
@@ -513,66 +671,127 @@
                 back_send[i, a, m, per:] = im
 
         loop(0, count, gather)
-        back_recv[i, me] = back_send[i, me]
-        loop(1, n, lambda o: home(i, o).start())
-
-    for i in range(chunks):
-        column_chunk(i)
-
-    for i in range(chunks):
-        loop(1, n, lambda o: home(i, o).wait_recv())
-
-        def column(m):
-            got = dot_left(row_inv, jnp.concatenate([back_recv[i, j, m] for j in range(n)], axis=0))
-            work[i * count + m] = got.reshape(2, LANES, LANES)
-
-        loop(0, count, column)
-
-    def gather_rows(t):
+        pl.when(jnp.logical_and(i == 0, lead))(fix_out)
+        for b in range(2):
+            back_recv[i, b, gi] = back_send[i, slabs[b]]
+        loop(1, g, lambda o: home(i, 1, o).start())
+
+    loop(0, chunks, column_chunk)
+    loop(0, chunks, lambda i: loop(1, g, lambda o: home(i, 0, o).start()))
+    loop(0, n_row, lambda e: x_back(e).wait_recv())
+
+    def take_chunk(i, b):
+        loop(1, g, lambda o: home(i, b, o).wait_recv())
+
+        def columns(t):
+            m = t * batch
+            parts = []
+            for k in range(batch):
+                parts.append(jnp.concatenate([back_recv[i, b, d, m + k] for d in range(g)], axis=0).T)
+            got = row_dots(jnp.concatenate(parts, axis=0), row_inv, slice(None))
+            work[pl.ds(i * count + m, batch)] = got.reshape(batch, LANES, 2 * LANES)
+
+        loop(0, count // batch, columns)
+
+    def take_extras(b):
+        parts = [xb_recv[e, 2 * b : 2 * b + 2, :] for e in range(n_row)]
+        parts.append(jnp.zeros((LANES - 2 * n_row, LANES), jnp.float32))
+        x = jnp.concatenate(parts, axis=0).T
+        hi, lo = split(x)
+        first, second = row_inv[2 + h, 0], row_inv[2 + h, 1]
+        work[0] = work[0] + (dot(hi, first) + (dot(lo, first) + dot(hi, second)))
+
+    def back_strip(t):
         at = pl.ds(pl.multiple_of(t * 8, 8), 8)
-        cos_rows, sin_rows = wide_cos[at, :], wide_sin[at, :]
-        zs = [
-            rotate(work[m, 0, at, :], work[m, 1, at, :], cos_rows[:, m : m + 1], -sin_rows[:, m : m + 1])
-            for m in range(low)
-        ]
-        for a, (re, im) in enumerate(cut_inverse(zs)):
-            turned[a, 0, at, :] = re
-            turned[a, 1, at, :] = im
-
-    loop(0, LANES // 8, gather_rows)
+
+        def entry(m):
+            re, im = work[m, at, :LANES], work[m, at, LANES:]
+            return rotate(re, im, tall_cos[m : m + 1, :], -tall_sin[m : m + 1, :])
+
+        pairs = {}
+        for m in real_names(low):
+            re, im = entry(m)
+            if m in (0, half):
+                pairs[m] = (re, None)
+            else:
+                re_too, im_too = entry(low - m)
+                pairs[m] = (re + re_too, im - im_too)
+        return at, real_cut(pairs, low)
+
+    loop(0, chunks, lambda i: take_chunk(i, 1))
+    take_extras(1)
+
+    def img_piece(p):
+        def strip(t):
+            at, xs = back_strip(t)
+            for a, x in enumerate(xs):
+                img_send[at, a * LANES : (a + 1) * LANES] = x
+
+        loop(p * (step_rows // 8), (p + 1) * (step_rows // 8), strip)
+        img_copy(p).start()
+
+    loop(0, pieces, img_piece)
+    loop(0, chunks, lambda i: take_chunk(i, 0))
+    take_extras(0)
     load_res.wait()
     noise = noise_ref[0]
-    for c in range(2):
-        totals = [jnp.zeros((8, LANES), jnp.float32)] * 4
+
+    def tally(c, at, a, applied, totals):
+        cs = slice(a * LANES, (a + 1) * LANES)
+        d, r = dir_ref[c, at, cs], res_ref[c, at, cs]
+        image = applied + noise * d
+        d_out[c, at, cs] = image
+        terms = (r * r, d * image, r * image, image * image)
+        return [total + term for total, term in zip(totals, terms)]
+
+    def own_strip(t, totals):
+        at, xs = back_strip(t)
+        for a, x in enumerate(xs):
+            totals = tally(h, at, a, x, totals)
+        return totals
+
+    def far_strip(t, totals):
+        at = pl.ds(pl.multiple_of(t * 8, 8), 8)
         for a in range(half):
-            at = slice(a * LANES, (a + 1) * LANES)
-            d, r = dir_ref[c, :, at], res_ref[c, :, at]
-            image = turned[a, c].T + noise * d
-            d_out[c, :, at] = image
-            for s, term in enumerate((r * r, d * image, r * image, image * image)):
-                totals[s] = totals[s] + jnp.sum(term.reshape(LANES // 8, 8, LANES), axis=0)
+            totals = tally(1 - h, at, a, img_in[at, a * LANES : (a + 1) * LANES], totals)
+        return totals
+
+    zeros = [jnp.zeros((8, LANES), jnp.float32)] * 4
+
+    def keep(c, totals):
         for s in range(4):
-            sums_ref[4 * c + s : 4 * c + s + 1, :] = jnp.sum(totals[s], axis=0, keepdims=True)
+            sums_ref[c, s : s + 1, :] = jnp.sum(totals[s], axis=0, keepdims=True)
+
+    sums_ref[...] = jnp.zeros_like(sums_ref)
+    keep(h, lax.fori_loop(0, LANES // 8, own_strip, zeros))
+
+    def far_piece(p, totals):
+        img_copy(p).wait_recv()
+        return lax.fori_loop(p * (step_rows // 8), (p + 1) * (step_rows // 8), far_strip, totals)
+
+    keep(1 - h, lax.fori_loop(0, pieces, far_piece, zeros))
 
     def share(o):
-        return pltpu.make_async_remote_copy(
-            src_ref=sums_ref,
-            dst_ref=held.at[me],
-            send_sem=sum_send_sem.at[o],
-            recv_sem=sum_recv_sem.at[o],
-            device_id=place(o)[1],
-            device_id_type=MESH,
-        )
+        return remote(sums_ref, held.at[me], sum_ssem.at[o], sum_rsem.at[o], place(o))
 
     held[me] = sums_ref[...]
     loop(1, n, lambda o: share(o).start())
-    for i in range(chunks):
-        loop(1, n, lambda o: ahead(i, o).wait_send())
-        loop(1, n, lambda o: home(i, o).wait_send())
+
+    def drain(i):
+        for b in range(2):
+            loop(1, g, lambda o: ahead(i, b, o).wait_send())
+            loop(1, g, lambda o: home(i, b, o).wait_send())
+
+    loop(0, chunks, drain)
+    loop(0, n_row, lambda e: x_ahead(e).wait_send())
+    pl.when(lead)(lambda: loop(0, g, lambda d: x_home(d).wait_send()))
+    loop(0, pieces, lambda p: raw_copy(p).wait_send())
+    loop(0, pieces, lambda p: img_copy(p).wait_send())
     loop(1, n, lambda o: share(o).wait())
-    total = jnp.sum(jnp.sum(held[...], axis=0), axis=1, keepdims=True)
+    total = jnp.sum(held[...], axis=0)
     for c in range(2):
-        old, curve, cross, square = [total[4 * c + s : 4 * c + s + 1] for s in range(4)]
+        line = jnp.sum(total[c], axis=1, keepdims=True)
+        old, curve, cross, square = [line[s : s + 1] for s in range(4)]
         step = old / curve
         new = jnp.maximum(old - 2.0 * step * cross + step * step * square, 0.0)
         beta = new / (old + TINY)
@@ -587,47 +806,88 @@
         loop(0, LANES // 8, strip)
 
 
-def fused_body(n_row, n_sub, residual_in, direction, spectrum, noise_var):
+def half_tables(embed, n_row, n_sub):
+    low, n, hs = embed // LANES, n_row * n_sub, n_sub // 2
+    per = LANES // n
+    slots = np.arange(LANES)
+    scale = 2.0 / (embed * embed)
+    fwd_all, inv_all, inv_extra = [], [], []
+    for part in range(2):
+        own = [r * n_sub + part * hs + s for r in range(n_row) for s in range(hs)]
+        freqs = np.stack([per * j + np.arange(per) for j in own])
+        extra = np.array([per * (r * n_sub + (1 - part) * hs) for r in range(n_row)])[:, None]
+
+        def forward(q):
+            block = complex_block(*unit(slots[:, None] * q.reshape(-1)[None, :], LANES, -1.0))
+            block = block.reshape(2, LANES, 2, *q.shape).transpose(0, 1, 3, 2, 4).reshape(2 * LANES, -1)
+            return np.pad(block, ((0, 0), (0, LANES - block.shape[1])))
+
+        def inverse(q):
+            block = complex_block(*unit(q.reshape(-1)[:, None] * slots[None, :], LANES, 1.0))
+            block = block.reshape(2, *q.shape, 2 * LANES).transpose(1, 0, 2, 3).reshape(-1, 2 * LANES)
+            return np.pad(block * scale, ((0, LANES - block.shape[0]), (0, 0)))
+
+        fwd_all.append(halves(np.concatenate([forward(freqs), forward(extra)], axis=1)))
+        inv_all.append(halves(inverse(freqs)))
+        inv_extra.append(halves(inverse(extra)))
+    return jnp.stack(fwd_all), jnp.stack(inv_all + inv_extra)
+
+
+def half_body(n_row, n_sub, residual_in, direction, spectrum, noise_var):
     _, rows, grid_len = direction.shape
     embed = 2 * grid_len
-    low, half = embed // LANES, grid_len // LANES
+    low = embed // LANES
     n = n_row * n_sub
+    g = n // 2
     per = LANES // n
     f32 = jnp.float32
     vmem = pl.BlockSpec(memory_space=pltpu.VMEM)
     away = pl.BlockSpec(memory_space=pl.ANY)
-    chunks = CHUNKS
+    chunks, pieces = CHUNKS, PIECES
     count = low // chunks
-    tables = make_tables(embed, n, per)
-    block = pltpu.VMEM((chunks, n, count, 2 * per, LANES), f32)
-    flags = pltpu.SemaphoreType.DMA((chunks, n))
+    lanes = spectrum.shape[1]
+    row_fwd, row_inv = half_tables(embed, n_row, n_sub)
+    _, _, col_fwd, col_inv, _, _, tall_cos, tall_sin = make_tables(embed, n, per)
+    col_inv = halves(complex_block(*unit(np.arange(LANES)[:, None] * np.arange(LANES)[None, :], LANES, 1.0)).reshape(2 * LANES, 2 * LANES))
+    tile = (count, 2 * per, LANES)
+    dma = pltpu.SemaphoreType.DMA
     residual_out, direction_out, steps = pl.pallas_call(
-        functools.partial(fused_kernel, low, chunks, n_row, n_sub),
+        functools.partial(half_kernel, low, chunks, pieces, n_row, n_sub),
         out_shape=[
             jax.ShapeDtypeStruct(direction.shape, f32),
             jax.ShapeDtypeStruct(direction.shape, f32),
             jax.ShapeDtypeStruct((2, LANES), f32),
         ],
-        in_specs=[vmem, away, away, pl.BlockSpec(memory_space=pltpu.SMEM)] + [vmem] * 8,
+        in_specs=[vmem, away, away, pl.BlockSpec(memory_space=pltpu.SMEM)] + [vmem] * 6,
         out_specs=[vmem] * 3,
         scratch_shapes=[
             pltpu.VMEM(direction.shape, f32),
-            pltpu.VMEM((spectrum.shape[1] // LANES, embed, LANES), f32),
-            pltpu.VMEM((low, spectrum.shape[1], LANES), f32),
-            pltpu.VMEM((low, 2, LANES, rows), f32),
-            pltpu.VMEM((half, 2, LANES, rows), f32),
+            pltpu.VMEM((lanes // LANES, embed, LANES), f32),
+            pltpu.VMEM((low, lanes, LANES), f32),
+            pltpu.VMEM((low, rows, 2 * LANES), f32),
             pltpu.VMEM((low, count, per, 2 * LANES), f32),
-            block, block, block, block,
-            pltpu.VMEM((n, 8, LANES), f32),
-            pltpu.VMEM((8, LANES), f32),
-            pltpu.SemaphoreType.DMA((1 + spectrum.shape[1] // LANES,)),
-            flags, flags, flags, flags,
-            pltpu.SemaphoreType.DMA((n,)),
-            pltpu.SemaphoreType.DMA((n,)),
+            pltpu.VMEM((chunks, 2, g, *tile), f32),
+            pltpu.VMEM((chunks, n, *tile), f32),
+            pltpu.VMEM((chunks, n, *tile), f32),
+            pltpu.VMEM((chunks, 2, g, *tile), f32),
+            pltpu.VMEM((rows, grid_len), f32),
+            pltpu.VMEM((rows, grid_len), f32),
+            pltpu.VMEM((rows, grid_len), f32),
+            pltpu.VMEM((n_row, 8, LANES), f32),
+            pltpu.VMEM((g, 8, LANES), f32),
+            pltpu.VMEM((g, 8, LANES), f32),
+            pltpu.VMEM((n_row, 8, LANES), f32),
+            pltpu.VMEM((n, 2, 8, LANES), f32),
+            pltpu.VMEM((2, 8, LANES), f32),
+            dma((1 + lanes // LANES,)),
+            dma((pieces,)), dma((pieces,)), dma((pieces,)), dma((pieces,)),
+            dma((chunks, 2, g)), dma((chunks, 2, g)), dma((chunks, 2, g)), dma((chunks, 2, g)),
+            dma((n_row,)), dma((g,)), dma((g,)), dma((n_row,)),
+            dma((n,)), dma((n,)),
         ],
         compiler_params=params(collective_id=1, has_side_effects=True),
         name="cg_step",
-    )(direction, residual_in, spectrum, noise_var, *tables)
+    )(direction, residual_in, spectrum, noise_var, row_fwd, row_inv, col_fwd, col_inv, tall_cos, tall_sin)
     return residual_out, direction_out, steps[:, 0]
 
 
@@ -638,8 +898,9 @@
         embed = spectrum.shape[0]
         low = embed // LANES
         per = LANES // (n_row * n_sub)
-        if direction.shape[1] == LANES and direction.shape[2] == LANES * n_row * n_sub and per % 8 == 0:
-            return fused_body(n_row, n_sub, residual_in, direction, spectrum, noise_var)
+        whole = direction.shape[1] == LANES and direction.shape[2] == LANES * n_row * n_sub
+        if whole and per % 8 == 0 and n_sub % 2 == 0:
+            return half_body(n_row, n_sub, residual_in, direction, spectrum, noise_var)
         weights = spectrum.reshape(LANES, low, per, low).transpose(1, 3, 2, 0)
         return pair_body(n_row, n_sub, residual_in, direction, weights, noise_var)
 

time: 215 us -> 168 us (0.78)
  Pallas kernels: 208 us -> 161 us
    pallas_call x1, Pallas kernels: 208 us -> 161 us  [half_body(): pl.pallas_call(functools.partial(half_kernel, low, chunks, pieces, n_row,...]
where the time goes in v1:
time: 168 us
  Pallas kernels  161 us (96%)
  local copies, waits for them, and re-layouts  5.89 us (4%)
    pallas_call x1, Pallas kernels, half_body(): pl.pallas_call(functools.partial(half_kernel, low, chunks, pieces, n_row,...  161 us
    unnamed x4, local copies, waits for them, and re-layouts  4.61 us

profile of v1, /device:TPU:0, one launch (start us, length us, event | category | flops | bytes accessed | tf_op | source)
XLA Modules:
  0.0 168.2 jit_solution(14412926170623739365)
XLA Ops:
  1.3 161.0 %cg_step.1 = (f32[2,128,2048]{2,1,0:T(8,128)}, f32[2,128,2048]{2,1,0:T(8,128)}, f32[2,128]{1,0:T(2,128)}) custom-call(f32[2,128,2048]{2,1,0:T(8,128)} %dir_ref.1, f32[2,128,2048]{2,1,0:T(8,128)} %res_hbm.1, f32[4096,256]{1,0:T(8,128)} %spec_hbm.1, f32[1]{0:T(128)S(6)} %copy.19.noise_ref, bf16[2,2,256,256]{3,2,1,0:T(8,128)(2,1)} %constant.33.row_fwd, ...), custom_call_target="tpu_custom_call" | custom-call | tf_op jit(solution)/shard_map/cg_step/pallas_call | solution.py:854
  162.3 1.3 slice_reduce_fusion
  163.6 0.0 copy-start
  163.6 3.3 %copy.20 = f32[2,128,2048]{2,1,0:T(8,128)} copy(f32[2,128,2048]{2,1,0:T(8,128)} %get-tuple-element.12) | data formatting | bytes 4194304
  166.9 0.0 copy-done
  166.9 1.3 copy.21
Async XLA Ops:
  163.6 3.3 %copy-start = (f32[2,128,2048]{2,1,0:T(8,128)S(1)}, f32[2,128,2048]{2,1,0:T(8,128)}, u32[]{:S(2)}) copy-start(f32[2,128,2048]{2,1,0:T(8,128)} %get-tuple-element.13) | copy-start | bytes 6291460

commit v2 on v1

--- a/solution.py
+++ b/solution.py
@@ -13,6 +13,7 @@
 TINY = 1e-06
 CHUNKS = 4
 PIECES = 4
+HALF_GRANT = 48 * 1024 * 1024
 MESH = pl.DeviceIdType.MESH
 GRANT = 60 * 1024 * 1024
 
@@ -446,9 +447,10 @@
 
 def half_kernel(
     low, chunks, pieces, n_row, n_sub,
-    dir_ref, res_hbm, spec_hbm, noise_ref, row_fwd, row_inv, col_fwd, col_inv, tall_cos, tall_sin,
-    r_out, d_out, s_out,
-    res_ref, spec_ref, weights, work, cols, send, recv, back_send, back_recv,
+    dir_hbm, res_hbm, spec_hbm, noise_ref, row_fwd_hbm, row_inv_hbm, col_fwd_hbm, col_inv_hbm, tall_cos, tall_sin,
+    image_ref, dir_ref, res_ref, coef_ref,
+    spec_ref, row_fwd, row_inv, col_fwd, col_inv,
+    weights, work, cols, send, recv, back_send, back_recv,
     raw_in, img_send, img_in, x_send, x_recv, xb_send, xb_recv, held, sums_ref,
     load_sem, raw_ssem, raw_rsem, img_ssem, img_rsem, send_sem, recv_sem, back_ssem, back_rsem,
     x_ssem, x_rsem, xb_ssem, xb_rsem, sum_ssem, sum_rsem,
@@ -486,11 +488,28 @@
         1, n,
         lambda o: pl.semaphore_signal(barrier, inc=1, device_id=place(o), device_id_type=MESH),
     )
-    load_res = pltpu.make_async_copy(res_hbm, res_ref, load_sem.at[0])
+
+    def load(src, dst, slot):
+        return pltpu.make_async_copy(src, dst, load_sem.at[slot])
+
+    load_dir = [load(dir_hbm.at[c], dir_ref.at[c], s) for s, c in enumerate((h, 1 - h))]
+    load_fwd = load(row_fwd_hbm, row_fwd, 2)
+    load_rest = [
+        load(src, dst, 3 + s)
+        for s, (src, dst) in enumerate(
+            ((row_inv_hbm, row_inv), (col_fwd_hbm, col_fwd), (col_inv_hbm, col_inv), (res_hbm, res_ref))
+        )
+    ]
     load_spec = [
-        pltpu.make_async_copy(spec_hbm.at[:, pl.ds(s * LANES, LANES)], spec_ref.at[s], load_sem.at[s + 1])
-        for s in range(spec_ref.shape[0])
+        load(spec_hbm.at[:, pl.ds(s * LANES, LANES)], spec_ref.at[s], 7 + s) for s in range(spec_ref.shape[0])
     ]
+    load_dir[0].start()
+    load_fwd.start()
+    for one in load_spec:
+        one.start()
+    for one in load_rest:
+        one.start()
+    load_dir[1].start()
 
     def remote(src, dst, s_sem, r_sem, device):
         return pltpu.make_async_remote_copy(
@@ -499,7 +518,7 @@
 
     def raw_copy(p):
         at = pl.ds(pl.multiple_of(p * step_rows, step_rows), step_rows)
-        return remote(dir_ref.at[1 - h, at, :], raw_in.at[at, :], raw_ssem.at[p], raw_rsem.at[p], mate)
+        return remote(dir_hbm.at[1 - h, at, :], raw_in.at[at, :], raw_ssem.at[p], raw_rsem.at[p], mate)
 
     def img_copy(p):
         at = pl.ds(pl.multiple_of(p * step_rows, step_rows), step_rows)
@@ -532,9 +551,6 @@
 
     pl.semaphore_wait(barrier, n - 1)
     loop(0, pieces, lambda p: raw_copy(p).start())
-    for load in load_spec:
-        load.start()
-    load_res.start()
 
     def row_strip(read, t):
         at = pl.ds(pl.multiple_of(t * 8, 8), 8)
@@ -576,12 +592,14 @@
         recv[i, slabs[b]] = send[i, b, gi]
         loop(1, g, lambda o: ahead(i, b, o).start())
 
+    load_dir[0].wait()
+    load_fwd.wait()
     loop(0, LANES // 8, lambda t: row_strip(lambda at, cs: dir_ref[h, at, cs], t))
     row_extras(0)
     loop(0, chunks, lambda i: send_chunk(i, 0))
 
-    for load in load_spec:
-        load.wait()
+    for one in load_spec:
+        one.wait()
 
     def turn_spectrum(k):
         for s in range(spec_ref.shape[0]):
@@ -589,6 +607,9 @@
             weights[k, s * LANES : (s + 1) * LANES, :] = part.T
 
     loop(0, low, turn_spectrum)
+    for one in load_rest:
+        one.wait()
+    load_dir[1].wait()
 
     def raw_piece(p):
         raw_copy(p).wait_recv()
@@ -733,14 +754,13 @@
     loop(0, pieces, img_piece)
     loop(0, chunks, lambda i: take_chunk(i, 0))
     take_extras(0)
-    load_res.wait()
     noise = noise_ref[0]
 
     def tally(c, at, a, applied, totals):
         cs = slice(a * LANES, (a + 1) * LANES)
         d, r = dir_ref[c, at, cs], res_ref[c, at, cs]
         image = applied + noise * d
-        d_out[c, at, cs] = image
+        image_ref[c, at, cs] = image
         terms = (r * r, d * image, r * image, image * image)
         return [total + term for total, term in zip(totals, terms)]
 
@@ -795,15 +815,44 @@
         step = old / curve
         new = jnp.maximum(old - 2.0 * step * cross + step * step * square, 0.0)
         beta = new / (old + TINY)
-        s_out[c : c + 1, :] = jnp.broadcast_to(step, (1, LANES))
+        coef_ref[c : c + 1, :] = jnp.broadcast_to(step, (1, LANES))
+        coef_ref[2 + c : 3 + c, :] = jnp.broadcast_to(beta, (1, LANES))
+
+
+def finish_kernel(parts, image_ref, dir_ref, res_ref, coef_ref, r_hbm, d_hbm, s_out, r_ref, d_ref, out_sem):
+    probes, rows = image_ref.shape[:2]
+    strip_rows = rows // parts
+
+    def stores(k):
+        at = pl.ds(pl.multiple_of(lax.rem(k, parts) * strip_rows, strip_rows), strip_rows)
+        return [
+            pltpu.make_async_copy(src.at[k // parts, at, :], dst.at[k // parts, at, :], out_sem.at[s, k])
+            for s, (src, dst) in enumerate(((r_ref, r_hbm), (d_ref, d_hbm)))
+        ]
+
+    for c in range(probes):
+        s_out[c] = coef_ref[c, 0]
+
+    def work(k):
+        c = k // parts
+        step, beta = coef_ref[pl.ds(c, 1), 0:1], coef_ref[pl.ds(c + 2, 1), 0:1]
 
         def strip(t):
-            at = pl.ds(pl.multiple_of(t * 8, 8), 8)
-            r = res_ref[c, at, :] - step * d_out[c, at, :]
-            r_out[c, at, :] = r
-            d_out[c, at, :] = r + beta * dir_ref[c, at, :]
-
-        loop(0, LANES // 8, strip)
+            at = pl.ds(pl.multiple_of(lax.rem(k, parts) * strip_rows + t * 8, 8), 8)
+            r = res_ref[c, at, :] - step * image_ref[c, at, :]
+            r_ref[c, at, :] = r
+            d_ref[c, at, :] = r + beta * dir_ref[c, at, :]
+
+        loop(0, strip_rows // 8, strip)
+        for one in stores(k):
+            one.start()
+
+    def drain(k):
+        for one in stores(k):
+            one.wait()
+
+    loop(0, probes * parts, work)
+    loop(0, probes * parts, drain)
 
 
 def half_tables(embed, n_row, n_sub):
@@ -851,18 +900,16 @@
     col_inv = halves(complex_block(*unit(np.arange(LANES)[:, None] * np.arange(LANES)[None, :], LANES, 1.0)).reshape(2 * LANES, 2 * LANES))
     tile = (count, 2 * per, LANES)
     dma = pltpu.SemaphoreType.DMA
-    residual_out, direction_out, steps = pl.pallas_call(
+    whole = pltpu.VMEM(direction.shape, f32)
+    kept = pltpu.VMEM(direction.shape, f32)
+    image, mine, rest, coef = pl.pallas_call(
         functools.partial(half_kernel, low, chunks, pieces, n_row, n_sub),
-        out_shape=[
-            jax.ShapeDtypeStruct(direction.shape, f32),
-            jax.ShapeDtypeStruct(direction.shape, f32),
-            jax.ShapeDtypeStruct((2, LANES), f32),
-        ],
-        in_specs=[vmem, away, away, pl.BlockSpec(memory_space=pltpu.SMEM)] + [vmem] * 6,
-        out_specs=[vmem] * 3,
+        out_shape=[kept, kept, kept, pltpu.VMEM((4, LANES), f32)],
+        in_specs=[away, away, away, pl.BlockSpec(memory_space=pltpu.SMEM)] + [away] * 4 + [vmem] * 2,
+        out_specs=[vmem] * 4,
         scratch_shapes=[
-            pltpu.VMEM(direction.shape, f32),
             pltpu.VMEM((lanes // LANES, embed, LANES), f32),
+            *[pltpu.VMEM(table.shape, table.dtype) for table in (row_fwd, row_inv, col_fwd, col_inv)],
             pltpu.VMEM((low, lanes, LANES), f32),
             pltpu.VMEM((low, rows, 2 * LANES), f32),
             pltpu.VMEM((low, count, per, 2 * LANES), f32),
@@ -879,16 +926,32 @@
             pltpu.VMEM((n_row, 8, LANES), f32),
             pltpu.VMEM((n, 2, 8, LANES), f32),
             pltpu.VMEM((2, 8, LANES), f32),
-            dma((1 + lanes // LANES,)),
+            dma((7 + lanes // LANES,)),
             dma((pieces,)), dma((pieces,)), dma((pieces,)), dma((pieces,)),
             dma((chunks, 2, g)), dma((chunks, 2, g)), dma((chunks, 2, g)), dma((chunks, 2, g)),
             dma((n_row,)), dma((g,)), dma((g,)), dma((n_row,)),
             dma((n,)), dma((n,)),
         ],
-        compiler_params=params(collective_id=1, has_side_effects=True),
+        compiler_params=pltpu.CompilerParams(
+            vmem_limit_bytes=HALF_GRANT, collective_id=1, has_side_effects=True
+        ),
         name="cg_step",
     )(direction, residual_in, spectrum, noise_var, row_fwd, row_inv, col_fwd, col_inv, tall_cos, tall_sin)
-    return residual_out, direction_out, steps[:, 0]
+    parts = PIECES
+    residual_out, direction_out, steps = pl.pallas_call(
+        functools.partial(finish_kernel, parts),
+        out_shape=[
+            jax.ShapeDtypeStruct(direction.shape, f32),
+            jax.ShapeDtypeStruct(direction.shape, f32),
+            jax.ShapeDtypeStruct((2,), f32),
+        ],
+        in_specs=[vmem] * 4,
+        out_specs=[away, away, pl.BlockSpec(memory_space=pltpu.SMEM)],
+        scratch_shapes=[whole, whole, dma((2, 2 * parts))],
+        compiler_params=pltpu.CompilerParams(vmem_limit_bytes=8 * 1024 * 1024),
+        name="finish",
+    )(*[pltpu.with_memory_space_constraint(x, pltpu.VMEM) for x in (image, mine, rest, coef)])
+    return residual_out, direction_out, steps
 
 
 def solution(mesh):

time: 168 us -> 161 us (0.958)
  local copies, waits for them, and re-layouts: 5.89 us -> 0 us
  Pallas kernels: 161 us -> 159 us
    unnamed x4 -> x0, local copies, waits for them, and re-layouts: 4.61 us -> none
    pallas_call x1, Pallas kernels: 161 us -> 156 us  [half_body(): pl.pallas_call(functools.partial(half_kernel, low, chunks, pieces, n_row,...]
    pallas_call x0 -> x1, Pallas kernels: none -> 3.04 us  [half_body(): pl.pallas_call(functools.partial(finish_kernel, parts), out_shape=[jax.Sh...]
where the time goes in v2:
time: 161 us
  Pallas kernels  159 us (99%)
    pallas_call x1, Pallas kernels, half_body(): pl.pallas_call(functools.partial(half_kernel, low, chunks, pieces, n_row,...  156 us

profile of v2, /device:TPU:0, one launch (start us, length us, event | category | flops | bytes accessed | tf_op | source)
XLA Modules:
  0.0 160.8 jit_solution(7133174500715784821)
XLA Ops:
  1.3 156.4 %cg_step.1 = (f32[2,128,2048]{2,1,0:T(8,128)S(1)}, f32[2,128,2048]{2,1,0:T(8,128)S(1)}, f32[2,128,2048]{2,1,0:T(8,128)S(1)}, f32[4,128]{1,0:T(4,128)S(1)}) custom-call(f32[2,128,2048]{2,1,0:T(8,128)} %dir_hbm.1, f32[2,128,2048]{2,1,0:T(8,128)} %res_hbm.1, f32[4096,256]{1,0:T(8,128)} %spec_hbm.1, f32[1]{0:T(128)S(6)} %copy.17.noise_ref, ...), custom_call_target="tpu_custom_call" | custom-call | tf_op jit(solution)/shard_map/cg_step/pallas_call | solution.py:905
  157.7 3.0 %finish.1 = (f32[2,128,2048]{2,1,0:T(8,128)}, f32[2,128,2048]{2,1,0:T(8,128)}, f32[2]{0:T(128)}) custom-call(f32[2,128,2048]{2,1,0:T(8,128)S(1)} %get-tuple-element.7.image_ref, f32[2,128,2048]{2,1,0:T(8,128)S(1)} %get-tuple-element.8.dir_ref, f32[2,128,2048]{2,1,0:T(8,128)S(1)} %get-tuple-element.9.res_ref, f32[4,128]{1,0:T(4,128)S(1)} %get-tuple-element.10.coef_ref), custom_call_target="tpu_custom_call" | custom-call | tf_op jit(solution)/shard_map/finish/pallas_call | solution.py:941

commit v3 on v2

--- a/solution.py
+++ b/solution.py
@@ -11,9 +11,9 @@
 
 LANES = 128
 TINY = 1e-06
-CHUNKS = 4
+CHUNKS = 8
 PIECES = 4
-HALF_GRANT = 48 * 1024 * 1024
+HALF_GRANT = 54 * 1024 * 1024
 MESH = pl.DeviceIdType.MESH
 GRANT = 60 * 1024 * 1024
 
@@ -453,11 +453,12 @@
     weights, work, cols, send, recv, back_send, back_recv,
     raw_in, img_send, img_in, x_send, x_recv, xb_send, xb_recv, held, sums_ref,
     load_sem, raw_ssem, raw_rsem, img_ssem, img_rsem, send_sem, recv_sem, back_ssem, back_rsem,
-    x_ssem, x_rsem, xb_ssem, xb_rsem, sum_ssem, sum_rsem,
+    x_sem, sum_sem,
 ):
     n = n_row * n_sub
     hs = n_sub // 2
     g = n_row * hs
+    held_rows = 3
     half = low // 2
     count = low // chunks
     per = LANES // n
@@ -467,9 +468,14 @@
     h = my_s // hs
     gi = my_r * hs + lax.rem(my_s, hs)
     me = my_r * n_sub + my_s
-    mate_s = n_sub - 1 - my_s
-    mate = {"row": my_r, "sub": mate_s}
-    slabs = [me, my_r * n_sub + mate_s]
+
+    def subs(part, own):
+        return [own, (n_sub - 1) * (1 - part), hs - part]
+
+    slabs = [my_r * n_sub + one for one in subs(h, my_s)]
+    inner = my_s == hs - 1 + h
+    tier = lax.rem(my_s + h, 2)
+    across = {"row": my_r, "sub": hs - h}
     lead = my_s == h * hs
 
     def place(o):
@@ -478,7 +484,17 @@
 
     def ally(d, part):
         r, s = d // hs, part * hs + lax.rem(d, hs)
-        return {"row": r, "sub": s}, [r * n_sub + s, r * n_sub + n_sub - 1 - s]
+        return {"row": r, "sub": s}, [r * n_sub + one for one in subs(part, s)]
+
+    def others(step):
+        loop(1, g, lambda o: step(lax.rem(gi + o, g)))
+
+    def inner_others(step):
+        def one(r):
+            p = r * hs + 1 - h
+            pl.when(p != gi)(lambda: step(p))
+
+        loop(0, n_row, one)
 
     def leader(e):
         return {"row": e, "sub": (1 - h) * hs}
@@ -516,38 +532,68 @@
             src_ref=src, dst_ref=dst, send_sem=s_sem, recv_sem=r_sem, device_id=device, device_id_type=MESH
         )
 
+    def strip_of(p):
+        return pl.ds(pl.multiple_of(p * step_rows, step_rows), step_rows)
+
     def raw_copy(p):
-        at = pl.ds(pl.multiple_of(p * step_rows, step_rows), step_rows)
-        return remote(dir_hbm.at[1 - h, at, :], raw_in.at[at, :], raw_ssem.at[p], raw_rsem.at[p], mate)
-
-    def img_copy(p):
-        at = pl.ds(pl.multiple_of(p * step_rows, step_rows), step_rows)
-        return remote(img_send.at[at, :], img_in.at[at, :], img_ssem.at[p], img_rsem.at[p], mate)
-
-    def ahead(i, b, o):
-        p = lax.rem(gi + o, g)
+        at = strip_of(p)
+        return remote(dir_hbm.at[1 - h, at, :], raw_in.at[tier, at, :], raw_ssem.at[0], raw_rsem.at[tier, p], across)
+
+    def raw_arrival(b, p):
+        at = strip_of(p)
         return remote(
-            send.at[i, b, p], recv.at[i, slabs[b]], send_sem.at[i, b, o], recv_sem.at[i, b, o], ally(p, h)[0]
+            dir_hbm.at[1 - h, at, :], raw_in.at[b - 1, at, :], raw_ssem.at[0], raw_rsem.at[b - 1, p], across
         )
 
-    def home(i, b, o):
-        p = lax.rem(gi + o, g)
+    def img_copy(b, p):
+        at = strip_of(p)
+        device = {"row": my_r, "sub": subs(h, my_s)[b]}
+        return remote(img_send.at[b - 1, at, :], img_in.at[at, :], img_ssem.at[0], img_rsem.at[p], device)
+
+    def img_arrival(p):
+        at = strip_of(p)
+        return remote(img_send.at[0, at, :], img_in.at[at, :], img_ssem.at[0], img_rsem.at[p], across)
+
+    def ahead(i, b, p):
+        return remote(
+            send.at[i, b, p], recv.at[i, slabs[b]], send_sem.at[i], recv_sem.at[i], ally(p, h)[0]
+        )
+
+    def gather_in(i, tiles):
+        return remote(recv.at[i, pl.ds(0, tiles)], recv.at[i, pl.ds(0, tiles)], send_sem.at[i], recv_sem.at[i], across)
+
+    def gone(i, held):
+        ref = send.at[i, pl.ds(0, held), pl.ds(0, g - 1)]
+        return remote(ref, ref, send_sem.at[i], recv_sem.at[i], across)
+
+    def back_gone(i, tiles):
+        ref = back_send.at[i, pl.ds(0, tiles)]
+        return remote(ref, ref, back_ssem.at[i], back_rsem.at[i, 0], across)
+
+    def home(i, b, p):
         device, places = ally(p, h)
         return remote(
-            back_send.at[i, places[b]], back_recv.at[i, b, gi], back_ssem.at[i, b, o], back_rsem.at[i, b, o], device
+            back_send.at[i, places[b]], back_recv.at[i, b, gi], back_ssem.at[i], back_rsem.at[i, b], device
         )
 
+    def back_arrival(i, b):
+        ref = back_recv.at[i, b, pl.ds(0, g - 1)]
+        return remote(ref, ref, back_ssem.at[i], back_rsem.at[i, b], across)
+
+    def either(step):
+        pl.when(inner)(lambda: step(True))
+        pl.when(jnp.logical_not(inner))(lambda: step(False))
+
+    alien = (held_rows - 1) * n_row + g - 1
+
     def x_ahead(e):
-        return remote(x_send.at[e], x_recv.at[gi], x_ssem.at[e], x_rsem.at[gi], leader(e))
-
-    def x_arrival(d):
-        return remote(x_send.at[0], x_recv.at[d], x_ssem.at[0], x_rsem.at[d], mate)
+        return remote(x_send.at[e], x_recv.at[gi], x_sem.at[0], x_sem.at[1], leader(e))
 
     def x_home(d):
-        return remote(xb_send.at[d], xb_recv.at[my_r], xb_ssem.at[d], xb_rsem.at[my_r], ally(d, 1 - h)[0])
-
-    def x_back(e):
-        return remote(xb_send.at[0], xb_recv.at[e], xb_ssem.at[0], xb_rsem.at[e], mate)
+        return remote(xb_send.at[d], xb_recv.at[my_r], x_sem.at[2], x_sem.at[3], ally(d, 1 - h)[0])
+
+    def x_all(ref, k):
+        return remote(ref, ref, x_sem.at[k], x_sem.at[k], across)
 
     pl.semaphore_wait(barrier, n - 1)
     loop(0, pieces, lambda p: raw_copy(p).start())
@@ -590,7 +636,7 @@
 
         loop(0, count // batch, columns)
         recv[i, slabs[b]] = send[i, b, gi]
-        loop(1, g, lambda o: ahead(i, b, o).start())
+        others(lambda p: ahead(i, b, p).start())
 
     load_dir[0].wait()
     load_fwd.wait()
@@ -598,6 +644,11 @@
     row_extras(0)
     loop(0, chunks, lambda i: send_chunk(i, 0))
 
+    def send_extras():
+        loop(0, n_row, lambda e: x_ahead(e).start())
+
+    pl.when(jnp.logical_not(inner))(send_extras)
+
     for one in load_spec:
         one.wait()
 
@@ -611,46 +662,64 @@
         one.wait()
     load_dir[1].wait()
 
-    def raw_piece(p):
-        raw_copy(p).wait_recv()
-        loop(
-            p * (step_rows // 8), (p + 1) * (step_rows // 8),
-            lambda t: row_strip(lambda at, cs: raw_in[at, cs], t),
-        )
-
-    loop(0, pieces, raw_piece)
-    row_extras(1)
-    loop(0, n_row, lambda e: x_ahead(e).start())
-    loop(0, chunks, lambda i: send_chunk(i, 1))
-
-    wide = 8
+    def far_rows():
+        for b in range(1, held_rows):
+
+            def raw_piece(p):
+                raw_arrival(b, p).wait_recv()
+                loop(
+                    p * (step_rows // 8), (p + 1) * (step_rows // 8),
+                    lambda t: row_strip(lambda at, cs: raw_in[b - 1, at, cs], t),
+                )
+
+            loop(0, pieces, raw_piece)
+            row_extras(b)
+            loop(0, chunks, lambda i: send_chunk(i, b))
+        send_extras()
+
+    pl.when(inner)(far_rows)
+
+    wide = 16
+
+    def foreign(d, step):
+        places = ally(d, 1 - h)[1]
+        step(0, places[0])
+
+        def rest():
+            for b in range(1, held_rows):
+                step(b, places[b])
+
+        pl.when(lax.rem(d, hs) == h)(rest)
 
     def fix_in():
         def one(d):
-            x_arrival(d).wait_recv()
-            for b, place_in in enumerate(ally(d, 1 - h)[1]):
+            def add_in(b, place_in):
                 re, im = x_recv[d, 2 * b : 2 * b + 1, :], x_recv[d, 2 * b + 1 : 2 * b + 2, :]
                 recv[0, place_in, 0, 0:1, :] = recv[0, place_in, 0, 0:1, :] - im
                 recv[0, place_in, 0, per : per + 1, :] = recv[0, place_in, 0, per : per + 1, :] + re
 
+            foreign(d, add_in)
+
+        x_all(x_recv, 1).wait_recv()
         loop(0, g, one)
 
     def fix_out():
         def one(d):
-            for b, place_in in enumerate(ally(d, 1 - h)[1]):
+            def take_out(b, place_in):
                 re = 0.5 * back_send[0, place_in, 0, 0:1, :]
                 im = 0.5 * back_send[0, place_in, 0, per : per + 1, :]
                 back_send[0, place_in, 0, 0:1, :] = re
                 back_send[0, place_in, 0, per : per + 1, :] = im
                 xb_send[d, 2 * b : 2 * b + 1, :] = im
                 xb_send[d, 2 * b + 1 : 2 * b + 2, :] = -re
+
+            foreign(d, take_out)
             x_home(d).start()
 
         loop(0, g, one)
 
     def column_chunk(i):
-        for b in range(2):
-            loop(1, g, lambda o: ahead(i, b, o).wait_recv())
+        either(lambda near: gather_in(i, alien - (held_rows - 1 if near else 0)).wait_recv())
         pl.when(jnp.logical_and(i == 0, lead))(fix_in)
 
         def spread(m):
@@ -693,16 +762,23 @@
 
         loop(0, count, gather)
         pl.when(jnp.logical_and(i == 0, lead))(fix_out)
-        for b in range(2):
+        for b in range(held_rows):
             back_recv[i, b, gi] = back_send[i, slabs[b]]
-        loop(1, g, lambda o: home(i, 1, o).start())
+
+        def first(p):
+            near = lax.rem(p + h, hs) == 1
+            pl.when(near)(lambda: home(i, 1, p).start())
+            pl.when(jnp.logical_not(near))(lambda: home(i, 0, p).start())
+
+        others(first)
 
     loop(0, chunks, column_chunk)
-    loop(0, chunks, lambda i: loop(1, g, lambda o: home(i, 0, o).start()))
-    loop(0, n_row, lambda e: x_back(e).wait_recv())
+    for b in (2, 0):
+        loop(0, chunks, lambda i: inner_others(lambda p: home(i, b, p).start()))
+    x_all(xb_recv, 3).wait_recv()
 
     def take_chunk(i, b):
-        loop(1, g, lambda o: home(i, b, o).wait_recv())
+        back_arrival(i, b).wait_recv()
 
         def columns(t):
             m = t * batch
@@ -739,19 +815,23 @@
                 pairs[m] = (re + re_too, im - im_too)
         return at, real_cut(pairs, low)
 
-    loop(0, chunks, lambda i: take_chunk(i, 1))
-    take_extras(1)
-
-    def img_piece(p):
-        def strip(t):
-            at, xs = back_strip(t)
-            for a, x in enumerate(xs):
-                img_send[at, a * LANES : (a + 1) * LANES] = x
-
-        loop(p * (step_rows // 8), (p + 1) * (step_rows // 8), strip)
-        img_copy(p).start()
-
-    loop(0, pieces, img_piece)
+    def far_back():
+        for b in range(1, held_rows):
+            loop(0, chunks, lambda i: take_chunk(i, b))
+            take_extras(b)
+
+            def img_piece(p):
+                def strip(t):
+                    at, xs = back_strip(t)
+                    for a, x in enumerate(xs):
+                        img_send[b - 1, at, a * LANES : (a + 1) * LANES] = x
+
+                loop(p * (step_rows // 8), (p + 1) * (step_rows // 8), strip)
+                img_copy(b, p).start()
+
+            loop(0, pieces, img_piece)
+
+    pl.when(inner)(far_back)
     loop(0, chunks, lambda i: take_chunk(i, 0))
     take_extras(0)
     noise = noise_ref[0]
@@ -786,28 +866,32 @@
     keep(h, lax.fori_loop(0, LANES // 8, own_strip, zeros))
 
     def far_piece(p, totals):
-        img_copy(p).wait_recv()
+        img_arrival(p).wait_recv()
         return lax.fori_loop(p * (step_rows // 8), (p + 1) * (step_rows // 8), far_strip, totals)
 
     keep(1 - h, lax.fori_loop(0, pieces, far_piece, zeros))
 
     def share(o):
-        return remote(sums_ref, held.at[me], sum_ssem.at[o], sum_rsem.at[o], place(o))
+        return remote(sums_ref, held.at[me], sum_sem.at[0], sum_sem.at[1], place(o))
 
     held[me] = sums_ref[...]
     loop(1, n, lambda o: share(o).start())
 
-    def drain(i):
-        for b in range(2):
-            loop(1, g, lambda o: ahead(i, b, o).wait_send())
-            loop(1, g, lambda o: home(i, b, o).wait_send())
-
-    loop(0, chunks, drain)
-    loop(0, n_row, lambda e: x_ahead(e).wait_send())
-    pl.when(lead)(lambda: loop(0, g, lambda d: x_home(d).wait_send()))
-    loop(0, pieces, lambda p: raw_copy(p).wait_send())
-    loop(0, pieces, lambda p: img_copy(p).wait_send())
-    loop(1, n, lambda o: share(o).wait())
+    def drain(near):
+        def one(i):
+            gone(i, held_rows if near else 1).wait_send()
+            back_gone(i, alien - (held_rows - 1 if near else 0)).wait_send()
+
+        loop(0, chunks, one)
+
+    either(drain)
+    x_all(x_send, 0).wait_send()
+    pl.when(lead)(lambda: x_all(xb_send, 2).wait_send())
+    remote(img_in, img_in, raw_ssem.at[0], raw_ssem.at[0], across).wait_send()
+
+    pl.when(inner)(lambda: remote(img_send, img_send, img_ssem.at[0], img_ssem.at[0], across).wait_send())
+    all_sums = held.at[pl.ds(0, n - 1)]
+    remote(all_sums, all_sums, sum_sem.at[0], sum_sem.at[1], across).wait()
     total = jnp.sum(held[...], axis=0)
     for c in range(2):
         line = jnp.sum(total[c], axis=1, keepdims=True)
@@ -826,7 +910,7 @@
     def stores(k):
         at = pl.ds(pl.multiple_of(lax.rem(k, parts) * strip_rows, strip_rows), strip_rows)
         return [
-            pltpu.make_async_copy(src.at[k // parts, at, :], dst.at[k // parts, at, :], out_sem.at[s, k])
+            pltpu.make_async_copy(src.at[k // parts, at, :], dst.at[k // parts, at, :], out_sem.at[s])
             for s, (src, dst) in enumerate(((r_ref, r_hbm), (d_ref, d_hbm)))
         ]
 
@@ -847,12 +931,9 @@
         for one in stores(k):
             one.start()
 
-    def drain(k):
-        for one in stores(k):
-            one.wait()
-
     loop(0, probes * parts, work)
-    loop(0, probes * parts, drain)
+    pltpu.make_async_copy(r_ref, r_hbm, out_sem.at[0]).wait()
+    pltpu.make_async_copy(d_ref, d_hbm, out_sem.at[1]).wait()
 
 
 def half_tables(embed, n_row, n_sub):
@@ -913,12 +994,12 @@
             pltpu.VMEM((low, lanes, LANES), f32),
             pltpu.VMEM((low, rows, 2 * LANES), f32),
             pltpu.VMEM((low, count, per, 2 * LANES), f32),
-            pltpu.VMEM((chunks, 2, g, *tile), f32),
+            pltpu.VMEM((chunks, 3, g, *tile), f32),
             pltpu.VMEM((chunks, n, *tile), f32),
             pltpu.VMEM((chunks, n, *tile), f32),
-            pltpu.VMEM((chunks, 2, g, *tile), f32),
-            pltpu.VMEM((rows, grid_len), f32),
-            pltpu.VMEM((rows, grid_len), f32),
+            pltpu.VMEM((chunks, 3, g, *tile), f32),
+            pltpu.VMEM((2, rows, grid_len), f32),
+            pltpu.VMEM((2, rows, grid_len), f32),
             pltpu.VMEM((rows, grid_len), f32),
             pltpu.VMEM((n_row, 8, LANES), f32),
             pltpu.VMEM((g, 8, LANES), f32),
@@ -927,10 +1008,9 @@
             pltpu.VMEM((n, 2, 8, LANES), f32),
             pltpu.VMEM((2, 8, LANES), f32),
             dma((7 + lanes // LANES,)),
-            dma((pieces,)), dma((pieces,)), dma((pieces,)), dma((pieces,)),
-            dma((chunks, 2, g)), dma((chunks, 2, g)), dma((chunks, 2, g)), dma((chunks, 2, g)),
-            dma((n_row,)), dma((g,)), dma((g,)), dma((n_row,)),
-            dma((n,)), dma((n,)),
+            dma((1,)), dma((2, pieces)), dma((1,)), dma((pieces,)),
+            dma((chunks,)), dma((chunks,)), dma((chunks,)), dma((chunks, 3)),
+            dma((4,)), dma((2,)),
         ],
         compiler_params=pltpu.CompilerParams(
             vmem_limit_bytes=HALF_GRANT, collective_id=1, has_side_effects=True
@@ -947,7 +1027,7 @@
         ],
         in_specs=[vmem] * 4,
         out_specs=[away, away, pl.BlockSpec(memory_space=pltpu.SMEM)],
-        scratch_shapes=[whole, whole, dma((2, 2 * parts))],
+        scratch_shapes=[whole, whole, dma((2,))],
         compiler_params=pltpu.CompilerParams(vmem_limit_bytes=8 * 1024 * 1024),
         name="finish",
     )(*[pltpu.with_memory_space_constraint(x, pltpu.VMEM) for x in (image, mine, rest, coef)])
@@ -962,7 +1042,7 @@
         low = embed // LANES
         per = LANES // (n_row * n_sub)
         whole = direction.shape[1] == LANES and direction.shape[2] == LANES * n_row * n_sub
-        if whole and per % 8 == 0 and n_sub % 2 == 0:
+        if whole and per % 8 == 0 and n_sub == 4:
             return half_body(n_row, n_sub, residual_in, direction, spectrum, noise_var)
         weights = spectrum.reshape(LANES, low, per, low).transpose(1, 3, 2, 0)
         return pair_body(n_row, n_sub, residual_in, direction, weights, noise_var)

time: 161 us -> 150 us (0.932)
  Pallas kernels: 159 us -> 149 us
    pallas_call x1, Pallas kernels: 156 us -> 146 us  [half_body(): pl.pallas_call(functools.partial(half_kernel, low, chunks, pieces, n_row,...]
where the time goes in v3:
time: 150 us
  Pallas kernels  149 us (99%)
    pallas_call x1, Pallas kernels, half_body(): pl.pallas_call(functools.partial(half_kernel, low, chunks, pieces, n_row,...  146 us

profile of v3, /device:TPU:0, one launch (start us, length us, event | category | flops | bytes accessed | tf_op | source)
XLA Modules:
  0.0 150.0 jit_solution(12892743186688584520)
XLA Ops:
  1.3 145.8 %cg_step.1 = (f32[2,128,2048]{2,1,0:T(8,128)S(1)}, f32[2,128,2048]{2,1,0:T(8,128)S(1)}, f32[2,128,2048]{2,1,0:T(8,128)S(1)}, f32[4,128]{1,0:T(4,128)S(1)}) custom-call(f32[2,128,2048]{2,1,0:T(8,128)} %dir_hbm.1, f32[2,128,2048]{2,1,0:T(8,128)} %res_hbm.1, f32[4096,256]{1,0:T(8,128)} %spec_hbm.1, f32[1]{0:T(128)S(6)} %copy.17.noise_ref, ...), custom_call_target="tpu_custom_call" | custom-call | tf_op jit(solution)/shard_map/cg_step/pallas_call | solution.py:986
  147.0 2.9 %finish.1 = (f32[2,128,2048]{2,1,0:T(8,128)}, f32[2,128,2048]{2,1,0:T(8,128)}, f32[2]{0:T(128)}) custom-call(f32[2,128,2048]{2,1,0:T(8,128)S(1)} %get-tuple-element.7.image_ref, f32[2,128,2048]{2,1,0:T(8,128)S(1)} %get-tuple-element.8.dir_ref, f32[2,128,2048]{2,1,0:T(8,128)S(1)} %get-tuple-element.9.res_ref, f32[4,128]{1,0:T(4,128)S(1)} %get-tuple-element.10.coef_ref), custom_call_target="tpu_custom_call" | custom-call | tf_op jit(solution)/shard_map/finish/pallas_call | solution.py:1021

commit v4 on v3

--- a/solution.py
+++ b/solution.py
@@ -655,7 +655,10 @@
     def turn_spectrum(k):
         for s in range(spec_ref.shape[0]):
             part = spec_ref[s, pl.ds(k, LANES, stride=low), :]
-            weights[k, s * LANES : (s + 1) * LANES, :] = part.T
+            turned = part.T
+            for q in range(LANES // low):
+                at = pl.ds(s * (LANES // low) + q, low, stride=per)
+                weights[k, at, :] = turned[q * low : (q + 1) * low]
 
     loop(0, low, turn_spectrum)
     for one in load_rest:
@@ -679,7 +682,7 @@
 
     pl.when(inner)(far_rows)
 
-    wide = 16
+    wide, twin = 16, 1
 
     def foreign(d, step):
         places = ally(d, 1 - h)[1]
@@ -732,17 +735,10 @@
         loop(0, count, spread)
         block = count * per
 
-        def filtered(t):
-            k = t * wide
+        def piece(k):
             spectral = dot_right(cols[pl.ds(k, wide)].reshape(wide * block, 2 * LANES), col_fwd)
-            scale = jnp.concatenate(
-                [
-                    weights[k + w, pl.ds(i * count + m, per, stride=low), :]
-                    for w in range(wide)
-                    for m in range(count)
-                ],
-                axis=0,
-            )
+            scale = weights[pl.ds(k, wide), pl.ds(pl.multiple_of(i * block, block), block), :]
+            scale = scale.reshape(wide * block, LANES)
             spectral = spectral * jnp.concatenate([scale, scale], axis=1)
             got = dot_right(spectral, col_inv)
             for w in range(wide):
@@ -752,7 +748,11 @@
                 cols[k + w, :, :, :LANES] = re.reshape(count, per, LANES)
                 cols[k + w, :, :, LANES:] = im.reshape(count, per, LANES)
 
-        loop(0, low // wide, filtered)
+        def filtered(t):
+            for one in range(twin):
+                piece((t * twin + one) * wide)
+
+        loop(0, low // (wide * twin), filtered)
 
         def gather(m):
             zs = [(cols[k, m, :, :LANES], cols[k, m, :, LANES:]) for k in range(low)]
@@ -858,9 +858,12 @@
 
     zeros = [jnp.zeros((8, LANES), jnp.float32)] * 4
 
+    lane = lax.broadcasted_iota(jnp.int32, (1, LANES), 1)
+
     def keep(c, totals):
         for s in range(4):
-            sums_ref[c, s : s + 1, :] = jnp.sum(totals[s], axis=0, keepdims=True)
+            one = jnp.sum(jnp.sum(totals[s], axis=0, keepdims=True), axis=1, keepdims=True)
+            sums_ref[...] = sums_ref[...] + jnp.where(lane == 4 * c + s, one, 0.0)
 
     sums_ref[...] = jnp.zeros_like(sums_ref)
     keep(h, lax.fori_loop(0, LANES // 8, own_strip, zeros))
@@ -894,8 +897,7 @@
     remote(all_sums, all_sums, sum_sem.at[0], sum_sem.at[1], across).wait()
     total = jnp.sum(held[...], axis=0)
     for c in range(2):
-        line = jnp.sum(total[c], axis=1, keepdims=True)
-        old, curve, cross, square = [line[s : s + 1] for s in range(4)]
+        old, curve, cross, square = [total[:, 4 * c + s : 4 * c + s + 1] for s in range(4)]
         step = old / curve
         new = jnp.maximum(old - 2.0 * step * cross + step * step * square, 0.0)
         beta = new / (old + TINY)
@@ -922,12 +924,12 @@
         step, beta = coef_ref[pl.ds(c, 1), 0:1], coef_ref[pl.ds(c + 2, 1), 0:1]
 
         def strip(t):
-            at = pl.ds(pl.multiple_of(lax.rem(k, parts) * strip_rows + t * 8, 8), 8)
+            at = pl.ds(pl.multiple_of(lax.rem(k, parts) * strip_rows + t * 16, 16), 16)
             r = res_ref[c, at, :] - step * image_ref[c, at, :]
             r_ref[c, at, :] = r
             d_ref[c, at, :] = r + beta * dir_ref[c, at, :]
 
-        loop(0, strip_rows // 8, strip)
+        loop(0, strip_rows // 16, strip)
         for one in stores(k):
             one.start()
 
@@ -1005,8 +1007,8 @@
             pltpu.VMEM((g, 8, LANES), f32),
             pltpu.VMEM((g, 8, LANES), f32),
             pltpu.VMEM((n_row, 8, LANES), f32),
-            pltpu.VMEM((n, 2, 8, LANES), f32),
-            pltpu.VMEM((2, 8, LANES), f32),
+            pltpu.VMEM((n, 1, LANES), f32),
+            pltpu.VMEM((1, LANES), f32),
             dma((7 + lanes // LANES,)),
             dma((1,)), dma((2, pieces)), dma((1,)), dma((pieces,)),
             dma((chunks,)), dma((chunks,)), dma((chunks,)), dma((chunks, 3)),

time: 150 us -> 149 us (level)
  Pallas kernels: 149 us -> 147 us
    pallas_call x1, Pallas kernels: 146 us -> 144 us  [half_body(): pl.pallas_call(functools.partial(half_kernel, low, chunks, pieces, n_row,...]
where the time goes in v4:
time: 149 us; the launch traced here: 148 us
  Pallas kernels  147 us (99%)
    pallas_call x1, Pallas kernels, half_body(): pl.pallas_call(functools.partial(half_kernel, low, chunks, pieces, n_row,...  144 us

profile of v4, /device:TPU:0, one launch (start us, length us, event | category | flops | bytes accessed | tf_op | source)
XLA Modules:
  0.0 148.2 jit_solution(13023398862472575176)
XLA Ops:
  1.3 144.2 %cg_step.1 = (f32[2,128,2048]{2,1,0:T(8,128)S(1)}, f32[2,128,2048]{2,1,0:T(8,128)S(1)}, f32[2,128,2048]{2,1,0:T(8,128)S(1)}, f32[4,128]{1,0:T(4,128)S(1)}) custom-call(f32[2,128,2048]{2,1,0:T(8,128)} %dir_hbm.1, f32[2,128,2048]{2,1,0:T(8,128)} %res_hbm.1, f32[4096,256]{1,0:T(8,128)} %spec_hbm.1, f32[1]{0:T(128)S(6)} %copy.17.noise_ref, ...), custom_call_target="tpu_custom_call" | custom-call | tf_op jit(solution)/shard_map/cg_step/pallas_call | solution.py:988
  145.5 2.7 %finish.1 = (f32[2,128,2048]{2,1,0:T(8,128)}, f32[2,128,2048]{2,1,0:T(8,128)}, f32[2]{0:T(128)}) custom-call(f32[2,128,2048]{2,1,0:T(8,128)S(1)} %get-tuple-element.7.image_ref, f32[2,128,2048]{2,1,0:T(8,128)S(1)} %get-tuple-element.8.dir_ref, f32[2,128,2048]{2,1,0:T(8,128)S(1)} %get-tuple-element.9.res_ref, f32[4,128]{1,0:T(4,128)S(1)} %get-tuple-element.10.coef_ref), custom_call_target="tpu_custom_call" | custom-call | tf_op jit(solution)/shard_map/finish/pallas_call | solution.py:1023

commit v5 on v4

--- a/solution.py
+++ b/solution.py
@@ -12,7 +12,7 @@
 LANES = 128
 TINY = 1e-06
 CHUNKS = 8
-PIECES = 4
+PIECES = 8
 HALF_GRANT = 54 * 1024 * 1024
 MESH = pl.DeviceIdType.MESH
 GRANT = 60 * 1024 * 1024
@@ -486,6 +486,9 @@
         r, s = d // hs, part * hs + lax.rem(d, hs)
         return {"row": r, "sub": s}, [r * n_sub + one for one in subs(part, s)]
 
+    def ordered(step):
+        loop(0, chunks, lambda t: step(t))
+
     def others(step):
         loop(1, g, lambda o: step(lax.rem(gi + o, g)))
 
@@ -642,7 +645,7 @@
     load_fwd.wait()
     loop(0, LANES // 8, lambda t: row_strip(lambda at, cs: dir_ref[h, at, cs], t))
     row_extras(0)
-    loop(0, chunks, lambda i: send_chunk(i, 0))
+    ordered(lambda i: send_chunk(i, 0))
 
     def send_extras():
         loop(0, n_row, lambda e: x_ahead(e).start())
@@ -677,8 +680,9 @@
 
             loop(0, pieces, raw_piece)
             row_extras(b)
-            loop(0, chunks, lambda i: send_chunk(i, b))
-        send_extras()
+            if b == held_rows - 1:
+                send_extras()
+            ordered(lambda i: send_chunk(i, b))
 
     pl.when(inner)(far_rows)
 
@@ -772,9 +776,9 @@
 
         others(first)
 
-    loop(0, chunks, column_chunk)
+    ordered(column_chunk)
     for b in (2, 0):
-        loop(0, chunks, lambda i: inner_others(lambda p: home(i, b, p).start()))
+        ordered(lambda i: inner_others(lambda p: home(i, b, p).start()))
     x_all(xb_recv, 3).wait_recv()
 
     def take_chunk(i, b):
@@ -817,7 +821,7 @@
 
     def far_back():
         for b in range(1, held_rows):
-            loop(0, chunks, lambda i: take_chunk(i, b))
+            ordered(lambda i: take_chunk(i, b))
             take_extras(b)
 
             def img_piece(p):
@@ -832,7 +836,7 @@
             loop(0, pieces, img_piece)
 
     pl.when(inner)(far_back)
-    loop(0, chunks, lambda i: take_chunk(i, 0))
+    ordered(lambda i: take_chunk(i, 0))
     take_extras(0)
     noise = noise_ref[0]
 

time: 149 us -> 149 us (level)
  no operation moved by 1% of the time
where the time goes in v5:
time: 149 us
  Pallas kernels  147 us (99%)
    pallas_call x1, Pallas kernels, half_body(): pl.pallas_call(functools.partial(half_kernel, low, chunks, pieces, n_row,...  145 us

profile of v5, /device:TPU:0, one launch (start us, length us, event | category | flops | bytes accessed | tf_op | source)
XLA Modules:
  0.0 148.7 jit_solution(17403776000577051256)
XLA Ops:
  1.3 144.8 %cg_step.1 = (f32[2,128,2048]{2,1,0:T(8,128)S(1)}, f32[2,128,2048]{2,1,0:T(8,128)S(1)}, f32[2,128,2048]{2,1,0:T(8,128)S(1)}, f32[4,128]{1,0:T(4,128)S(1)}) custom-call(f32[2,128,2048]{2,1,0:T(8,128)} %dir_hbm.1, f32[2,128,2048]{2,1,0:T(8,128)} %res_hbm.1, f32[4096,256]{1,0:T(8,128)} %spec_hbm.1, f32[1]{0:T(128)S(6)} %copy.17.noise_ref, ...), custom_call_target="tpu_custom_call" | custom-call | tf_op jit(solution)/shard_map/cg_step/pallas_call | solution.py:992
  146.1 2.6 %finish.1 = (f32[2,128,2048]{2,1,0:T(8,128)}, f32[2,128,2048]{2,1,0:T(8,128)}, f32[2]{0:T(128)}) custom-call(f32[2,128,2048]{2,1,0:T(8,128)S(1)} %get-tuple-element.7.image_ref, f32[2,128,2048]{2,1,0:T(8,128)S(1)} %get-tuple-element.8.dir_ref, f32[2,128,2048]{2,1,0:T(8,128)S(1)} %get-tuple-element.9.res_ref, f32[4,128]{1,0:T(4,128)S(1)} %get-tuple-element.10.coef_ref), custom_call_target="tpu_custom_call" | custom-call | tf_op jit(solution)/shard_map/finish/pallas_call | solution.py:1027
